TPU v7x, 32 devices: a whole 2x2x4 slice. The times are simulated.
32 devices in a mesh: row: 8 (over z, y), col: 4 (over x, core).
Axes of the slice: x: 2, y: 2, z: 4, core: 2. Of those that a mesh axis runs over, the one named last changes fastest.
Arguments:
- inputs: bfloat16 [4, 12288, 227], P(None, ('row', 'col')), may hold values from -6 to 6
- targets: bfloat16 [4, 12288, 83], P(None, ('row', 'col')), may hold values from -6 to 6
- cell_area: float32 [12288], P(('row', 'col')), may hold values from 0.1 to 1
- cell_count: int32 [32], P(('row', 'col')), may hold values from 128 to 384, as said below
- cell_node: int32 [12288], P(('row', 'col')), may hold values from 0 to 63
- edge_senders: int32 [32768], P(('row', 'col')), may hold values from 0 to 511
- edge_receivers: int32 [32768], P(('row', 'col')), may hold values from 0 to 255
- weight_input: float32 [227, 512], P(None, 'col'), may hold values from -0.375 to 0.375
- weight_latent: float32 [6, 512, 512], P(None, 'col'), may hold values from -0.25 to 0.25
- weight_output: float32 [512, 83], P('col'), may hold values from -0.25 to 0.25
- mean_input: float32 [227, 512], P(None, 'col'), may hold values from -0.00024414062 to 0.00024414062
- mean_latent: float32 [6, 512, 512], P(None, 'col'), may hold values from -0.00024414062 to 0.00024414062
- mean_output: float32 [512, 83], P('col'), may hold values from -0.00024414062 to 0.00024414062
- square_input: float32 [227, 512], P(None, 'col'), as said below
- square_latent: float32 [6, 512, 512], P(None, 'col'), as said below
- square_output: float32 [512, 83], P('col'), as said below
Outputs:
- loss_value: float32 [], replicated
- gradient_input: float32 [227, 512], P(None, 'col')
- gradient_latent: float32 [6, 512, 512], P(None, 'col')
- gradient_output: float32 [512, 83], P('col')
- first_input: float32 [227, 512], P(None, 'col')
- first_latent: float32 [6, 512, 512], P(None, 'col')
- first_output: float32 [512, 83], P('col')
- second_input: float32 [227, 512], P(None, 'col')
- second_latent: float32 [6, 512, 512], P(None, 'col')
- second_output: float32 [512, 83], P('col')
- master_input: float32 [227, 512], P(None, 'col')
- master_latent: float32 [6, 512, 512], P(None, 'col')
- master_output: float32 [512, 83], P('col')
- copy_input: bfloat16 [227, 512], P(None, 'col')
- copy_latent: bfloat16 [6, 512, 512], P(None, 'col')
- copy_output: bfloat16 [512, 83], P('col')
- trust_norms: float32 [2, 8], replicated
Inputs may be any that keep to these rules, and one draw needn't show every extreme that they name: `cell_count`: used cell slots of a device; some device uses all 384. `cell_node`: A node of the cell's own device. `edge_senders`: index into the block's column of nodes. `edge_receivers`: index into the block's row of nodes. `square_input`: Positive. `square_latent`: Positive. `square_output`: Positive.
All inputs are finite; a program needn't handle non-finite values.
Results may differ from a plain program's by a relative error of at most 0.0035.
The roundings to bfloat16 on the way count: a program that leaves them out, or rounds other values in their place, can miss the bound.
Values may be sent and summed in bfloat16 or wider, within the bound.
A program may use at most 192 MiB of HBM per device.

v0:
```python
import jax
import jax.numpy as jnp
from jax import lax
from jax.sharding import PartitionSpec as P

C_OUT = 83
DEG = 16
MESH_DEV = 64


highest = lax.Precision.HIGHEST
beta_first = 0.5
beta_second = 0.5
adam_epsilon = 1e-08
trust_epsilon = 1e-06
weight_decay = 0.01
learn_rate = 0.1


def silu_grad(pre_act, grad_out):
    sigma = jax.nn.sigmoid(pre_act)
    return grad_out * sigma * (1.0 + pre_act * (1.0 - sigma))


def reduced_matmul(form, left, right):
    return jnp.einsum(form, left, right, preferred_element_type=jnp.float32)


def split_parts(values):
    upper = values.astype(jnp.bfloat16)
    rest = values - upper.astype(jnp.float32)
    middle = rest.astype(jnp.bfloat16)
    lower = (rest - middle.astype(jnp.float32)).astype(jnp.bfloat16)
    return (upper, middle, lower)


def pick_rows(match, values):
    upper, middle, lower = split_parts(values)
    total = reduced_matmul("es,ksd->ked", match, upper)
    total = total + reduced_matmul("es,ksd->ked", match, middle)
    return total + reduced_matmul("es,ksd->ked", match, lower)


def add_into_rows(match, values):
    upper, middle, lower = split_parts(values)
    total = reduced_matmul("es,ked->ksd", match, upper)
    total = total + reduced_matmul("es,ked->ksd", match, middle)
    return total + reduced_matmul("es,ked->ksd", match, lower)


def one_hot_table(indices, count):
    return (indices[:, None] == jnp.arange(count, dtype=jnp.int32)[None, :]).astype(jnp.bfloat16)


def adam_parts(weight, gradient, first, second):
    new_first = beta_first * first + (1.0 - beta_first) * gradient
    new_second = beta_second * second + (1.0 - beta_second) * gradient * gradient
    update = new_first / (jnp.sqrt(new_second) + adam_epsilon) + weight_decay * weight
    return (new_first, new_second, update)


def body(
    inputs,
    targets,
    cell_area,
    cell_count,
    cell_node,
    edge_senders,
    edge_receivers,
    weight_input,
    weight_latent,
    weight_output,
    mean_input,
    mean_latent,
    mean_output,
    square_input,
    square_latent,
    square_output,
):
    full_input, complete_latent, full_output = (
        lax.all_gather(weight_input.astype(jnp.bfloat16), "col", axis=1, tiled=True),
        lax.all_gather(weight_latent.astype(jnp.bfloat16), "col", axis=1, tiled=True),
        lax.all_gather(weight_output.astype(jnp.bfloat16), "col", axis=0, tiled=True),
    )
    samples = inputs.shape[0]
    slots = inputs.shape[1]
    valid = (jnp.arange(slots, dtype=jnp.int32) < cell_count[0]).astype(jnp.float32)
    cell_weight = cell_area * valid
    area_total = lax.psum(jnp.sum(cell_weight), ("row", "col"))
    first_pre = reduced_matmul("sci,id->scd", inputs, full_input)
    grid_latent = jax.nn.silu(first_pre).astype(jnp.bfloat16)
    node_match = (cell_node[None, :] == jnp.arange(MESH_DEV, dtype=jnp.int32)[:, None]).astype(
        jnp.float32
    )
    node_match_low = node_match.astype(jnp.bfloat16)
    cell_match = node_match_low.T
    node_valid = node_match * valid[None, :]
    node_sum = reduced_matmul("nc,scd->snd", node_valid.astype(jnp.bfloat16), grid_latent)
    node_lower_limit = jnp.maximum(jnp.sum(node_valid, axis=1), 1.0)
    node_average = node_sum / node_lower_limit[None, :, None]
    average_reduced = node_average.astype(jnp.bfloat16)
    second_activation_input = reduced_matmul("kaj,jz->kaz", average_reduced, complete_latent[0])
    mesh_latent = jax.nn.silu(second_activation_input)
    mesh_state_reduced = mesh_latent.astype(jnp.bfloat16)
    receiver_local_part = reduced_matmul("kaj,jz->kaz", mesh_state_reduced, complete_latent[2])
    receiver_block = lax.all_gather(receiver_local_part, "col", axis=1, tiled=True)
    sender_block = reduced_matmul(
        "kaj,jz->kaz",
        lax.all_gather(mesh_state_reduced, "row", axis=1, tiled=True),
        complete_latent[1],
    )
    receiver_rows = receiver_block.shape[1]
    sender_rows = sender_block.shape[1]
    sender_match = one_hot_table(edge_senders, sender_rows)
    receiver_match = one_hot_table(edge_receivers, receiver_rows)
    edge_pre = pick_rows(sender_match, sender_block) + pick_rows(receiver_match, receiver_block)
    partial_sums = add_into_rows(receiver_match, jax.nn.silu(edge_pre))
    message_total = lax.psum_scatter(partial_sums, "col", scatter_dimension=1, tiled=True) / DEG
    message_total_reduced = message_total.astype(jnp.bfloat16)
    residual_branch = reduced_matmul("kaj,jz->kaz", message_total_reduced, complete_latent[3])
    mesh_next = mesh_latent + residual_branch
    decode_rows = reduced_matmul("cn,snd->scd", cell_match, mesh_next.astype(jnp.bfloat16)).astype(
        jnp.bfloat16
    )
    third_pre = reduced_matmul("scd,de->sce", decode_rows, complete_latent[4]) + reduced_matmul(
        "scd,de->sce", grid_latent, complete_latent[5]
    )
    grid_out = jax.nn.silu(third_pre).astype(jnp.bfloat16)
    predict = reduced_matmul("scd,do->sco", grid_out, full_output)
    error = predict - targets.astype(jnp.float32)
    denominator = C_OUT * samples * area_total
    weighted = cell_weight[None, :, None] * error
    loss_value = lax.psum(jnp.sum(weighted * error), ("row", "col")) / denominator
    d_predict = (2.0 * weighted / denominator).astype(jnp.bfloat16)
    grad_output_local = reduced_matmul("scd,sco->do", grid_out, d_predict)
    d_grid_out = reduced_matmul("sco,do->scd", d_predict, full_output)
    d_third = silu_grad(third_pre, d_grid_out).astype(jnp.bfloat16)
    grad_decode = reduced_matmul("scd,sce->de", decode_rows, d_third)
    grad_skip = reduced_matmul("scd,sce->de", grid_latent, d_third)
    d_decode = reduced_matmul("sce,de->scd", d_third, complete_latent[4])
    d_skip = reduced_matmul("sce,de->scd", d_third, complete_latent[5])
    d_mesh_next = jnp.einsum("nc,scd->snd", node_match, d_decode, precision=highest)
    residual_branch_gradient = d_mesh_next.astype(jnp.bfloat16)
    branch_gradient_sum = reduced_matmul(
        "lhg,lhj->gj", message_total_reduced, residual_branch_gradient
    )
    message_total_gradient = reduced_matmul(
        "pyk,ck->pyc", residual_branch_gradient, complete_latent[3]
    ).astype(jnp.bfloat16)
    d_block = lax.all_gather(message_total_gradient, "col", axis=1, tiled=True)
    d_edge_message = reduced_matmul("es,ksd->ked", receiver_match, d_block)
    d_edge_pre = silu_grad(edge_pre, d_edge_message / DEG)
    d_sender_part = add_into_rows(sender_match, d_edge_pre)
    d_receiver_part = add_into_rows(receiver_match, d_edge_pre)
    sender_gradient = lax.psum_scatter(
        d_sender_part.astype(jnp.bfloat16), "row", scatter_dimension=1, tiled=True
    )
    receiver_gradient = lax.psum_scatter(
        d_receiver_part.astype(jnp.bfloat16), "col", scatter_dimension=1, tiled=True
    )
    sender_weight_gradient = reduced_matmul("lhg,lhj->gj", mesh_state_reduced, sender_gradient)
    receiver_weight_gradient = reduced_matmul("lhg,lhj->gj", mesh_state_reduced, receiver_gradient)
    d_mesh = (
        d_mesh_next
        + reduced_matmul("pyk,ck->pyc", sender_gradient, complete_latent[1])
        + reduced_matmul("pyk,ck->pyc", receiver_gradient, complete_latent[2])
    )
    hidden_second_gradient = silu_grad(second_activation_input, d_mesh).astype(jnp.bfloat16)
    encoder_gradient = reduced_matmul("lhg,lhj->gj", average_reduced, hidden_second_gradient)
    node_average_gradient = (
        reduced_matmul("pyk,ck->pyc", hidden_second_gradient, complete_latent[0])
        / node_lower_limit[None, :, None]
    )
    d_grid = d_skip + valid[None, :, None] * pick_rows(cell_match, node_average_gradient)
    d_first = silu_grad(first_pre, d_grid).astype(jnp.bfloat16)
    grad_input_local = reduced_matmul("sci,scd->id", inputs, d_first)
    grad_latent_local = jnp.stack(
        [
            encoder_gradient,
            sender_weight_gradient,
            receiver_weight_gradient,
            branch_gradient_sum,
            grad_decode,
            grad_skip,
        ]
    )
    local_terms = (grad_input_local, grad_latent_local, grad_output_local)
    whole_input, whole_latent, whole_output = lax.psum(
        (local_terms[0], local_terms[1], local_terms[2]), ("row", "col")
    )
    column = lax.axis_index("col")
    width_input = weight_input.shape[1]
    width_latent = weight_latent.shape[1]
    width_output = weight_output.shape[0]
    gradient_input = lax.dynamic_slice_in_dim(whole_input, column * width_input, width_input, 1)
    gradient_latent = lax.dynamic_slice_in_dim(whole_latent, column * width_latent, width_latent, 1)
    gradient_output = lax.dynamic_slice_in_dim(whole_output, column * width_output, width_output, 0)
    first_input, second_input, update_input = adam_parts(
        weight_input, gradient_input, mean_input, square_input
    )
    first_latent, second_latent, update_latent = adam_parts(
        weight_latent, gradient_latent, mean_latent, square_latent
    )
    first_output, second_output, update_output = adam_parts(
        weight_output, gradient_output, mean_output, square_output
    )
    weight_sums = jnp.concatenate(
        [
            jnp.sum(weight_input * weight_input)[None],
            jnp.sum(weight_latent * weight_latent, axis=(1, 2)),
            jnp.sum(weight_output * weight_output)[None],
        ]
    )
    update_sums = jnp.concatenate(
        [
            jnp.sum(update_input * update_input)[None],
            jnp.sum(update_latent * update_latent, axis=(1, 2)),
            jnp.sum(update_output * update_output)[None],
        ]
    )
    norm_sums = lax.psum(jnp.stack([weight_sums, update_sums]), "col")
    trust_norms = jnp.sqrt(norm_sums)
    ratio = trust_norms[0] / (trust_norms[1] + trust_epsilon)
    master_input = weight_input - learn_rate * ratio[0] * update_input
    master_latent = weight_latent - learn_rate * ratio[1:7][:, None, None] * update_latent
    master_output = weight_output - learn_rate * ratio[7] * update_output
    return (
        loss_value,
        gradient_input,
        gradient_latent,
        gradient_output,
        first_input,
        first_latent,
        first_output,
        second_input,
        second_latent,
        second_output,
        master_input,
        master_latent,
        master_output,
        master_input.astype(jnp.bfloat16),
        master_latent.astype(jnp.bfloat16),
        master_output.astype(jnp.bfloat16),
        trust_norms,
    )


def solution(mesh):
    placed = (
        P(None, ("row", "col"), None),
        P(None, ("row", "col"), None),
        P(("row", "col")),
        P(("row", "col")),
        P(("row", "col")),
        P(("row", "col")),
        P(("row", "col")),
        P(None, "col"),
        P(None, "col", None),
        P("col", None),
        P(None, "col"),
        P(None, "col", None),
        P("col", None),
        P(None, "col"),
        P(None, "col", None),
        P("col", None),
    )
    return jax.shard_map(
        body,
        mesh=mesh,
        in_specs=placed,
        out_specs=(
            P(),
            P(None, "col"),
            P(None, "col", None),
            P("col", None),
            P(None, "col"),
            P(None, "col", None),
            P("col", None),
            P(None, "col"),
            P(None, "col", None),
            P("col", None),
            P(None, "col"),
            P(None, "col", None),
            P("col", None),
            P(None, "col"),
            P(None, "col", None),
            P("col", None),
            P(),
        ),
        check_vma=False,
    )
```

profile of v0, /device:TPU:0, one launch (start us, length us, event | category | flops | bytes accessed | tf_op | source)
XLA Modules:
  0.0 696.1 jit_solution(17898084965783241131)
XLA Ops:
  7.3 2.5 convert_element_type.186
  10.5 7.1 %all_gather.18 = bf16[227,512]{1,0:T(8,128)(2,1)S(1)} all-gather(bf16[227,128]{1,0:T(8,128)(2,1)S(1)} %convert_element_type.180), channel_id=1, replica_groups=mesh['row'=8,'col'=4] {'col'}, dimensions={1}, use_global_device_ids=true | all-gather | bytes 290560 | tf_op jit(solution)/shard_map/all_gather | solution.py:81
  17.7 2.7 multiply_convert_fusion.2
  22.0 19.5 %all-gather.5.cloned.1.call-done = bf16[6,512,512]{2,1,0:T(8,128)(2,1)} async-done(((bf16[6,128,512]{2,1,0:T(8,128)(2,1)}), bf16[6,512,512]{2,1,0:T(8,128)(2,1)}) %all-gather.5.cloned.1.call-update) | async-done | bytes 3145744 | tf_op jit(solution)/shard_map/all_gather | solution.py:82
  41.5 2.2 fusion.136
  43.7 2.2 fusion.112
  46.9 21.7 %all-gather.9.cloned.1.call-done = f32[4,256,512]{2,1,0:T(8,128)} async-done(((f32[4,64,512]{2,1,0:T(8,128)}), f32[4,256,512]{2,1,0:T(8,128)}) %all-gather.9.cloned.1.call-update) | async-done | bytes 2097168 | tf_op jit(solution)/shard_map/all_gather | solution.py:106
  68.7 6.5 fusion.46
  75.2 4.7 fusion.48
  79.9 40.0 %all-gather.7.cloned.1.call-done = bf16[4,512,512]{2,1,0:T(8,128)(2,1)} async-done(((bf16[4,64,512]{2,1,0:T(8,128)(2,1)}), bf16[4,512,512]{2,1,0:T(8,128)(2,1)}) %all-gather.7.cloned.1.call-update) | async-done | bytes 2097168 | tf_op jit(solution)/shard_map/all_gather | solution.py:109
  120.0 2.9 fusion.111
  122.9 5.9 fusion.24
  128.8 5.9 fusion.26
  134.7 5.9 fusion.28
  140.6 18.5 %add_add_fusion = f32[4,512,1024]{2,1,0:T(8,128)} fusion(f32[4,512,1024]{2,1,0:T(8,128)} %fusion.46, f32[4,512,1024]{2,1,0:T(8,128)} %fusion.48, f32[4,512,1024]{2,1,0:T(8,128)} %fusion.28, f32[4,512,1024]{2,1,0:T(8,128)} %fusion.24, f32[4,512,1024]{2,1,0:T(8,128)} %fusion.26, f32[4,256,512]{2,1,0:T(8,128)S(1)} %copy-done.1, s32[1024]{0:T(1024)S(1)} %copy-done.23), kind=kOutput, calls=%fused_computation.13 | convolution fusion | flops 1088159744 | bytes 52432896 | tf_op jit(solution)/shard_map/es,ksd->ked/dot_general | solution.py:26
  159.1 6.0 fusion.6
  165.1 2.5 fusion.8
  167.6 4.1 add_bitcast_fusion
  171.7 3.2 copy.56
  176.3 5.9 all_gather.22
  182.8 42.2 %all-reduce.10.cloned.1.call-done = f32[4,256,512]{2,0,1:T(4,128)} async-done(((f32[4,256,512]{2,0,1:T(4,128)}), f32[4,256,512]{2,0,1:T(4,128)}) %all-reduce.10.cloned.1.call-update) | async-done | bytes 2097168
  226.2 3.0 convolution_convert_fusion
  229.2 2.5 fusion.41
  231.8 3.0 multiply_convert_fusion.1
  236.0 1.2 fusion.95
  237.2 39.6 %all-reduce.3 = (f32[]{:T(128)}, f32[]{:T(128)}) all-reduce(f32[]{:T(128)} %get-tuple-element.53, f32[]{:T(128)} %get-tuple-element.43), channel_id=1, replica_groups=mesh['row'=8,'col'=4] {'row','col'}, use_global_device_ids=true, to_apply=%region_3.4 | all-reduce | flops 2 | bytes 16 | tf_op jit(solution)/shard_map/psum | solution.py:133
  277.5 3.3 multiply_convert_fusion
  280.8 2.1 fusion.113
  282.9 1.3 convolution_bitcast_fusion.5
  284.2 2.1 convolution_convert_fusion.1
  286.5 17.5 %all-gather.11.cloned.1.call-done = bf16[4,256,512]{2,1,0:T(8,128)(2,1)} async-done(((bf16[4,64,512]{2,1,0:T(8,128)(2,1)}), bf16[4,256,512]{2,1,0:T(8,128)(2,1)}) %all-gather.11.cloned.1.call-update) | async-done | bytes 1048592 | tf_op jit(solution)/shard_map/all_gather | solution.py:150
  304.0 6.5 fusion
  310.5 1.4 fusion.11
  312.0 1.4 fusion.81
  313.4 4.6 fusion.13
  318.0 4.5 fusion.18
  322.5 1.5 fusion.52
  324.0 1.8 copy.61
  326.1 12.4 %fusion.29 = bf16[4,512,512]{1,2,0:T(8,128)(2,1)} fusion(f32[4,512,512]{2,1,0:T(8,128)} %fusion.13, f32[4,512,512]{2,1,0:T(8,128)} %fusion.18, s32[1024]{0:T(1024)S(1)} %copy-done.30, f32[4,1024,512]{1,2,0:T(8,128)} %copy-done), kind=kOutput, calls=%fused_computation.45 | convolution fusion | flops 2165833728 | bytes 18878464 | tf_op jit(solution)/shard_map/es,ked->ksd/dot_general | solution.py:26
  338.5 4.6 copy.59
  344.4 2.4 convolution_bitcast_fusion.6
  346.8 15.5 %all-reduce.14.cloned.1.call-done = bf16[4,256,512]{2,0,1:T(4,128)(2,1)} async-done(((bf16[4,256,512]{2,0,1:T(4,128)(2,1)}), bf16[4,256,512]{2,0,1:T(4,128)(2,1)}) %all-reduce.14.cloned.1.call-update) | async-done | bytes 1048592
  363.3 105.4 %all-reduce.12.cloned.1.call-done = bf16[4,512,512]{2,0,1:T(4,128)(2,1)} async-done(((bf16[4,512,512]{2,0,1:T(4,128)(2,1)}), bf16[4,512,512]{2,0,1:T(4,128)(2,1)}) %all-reduce.12.cloned.1.call-update) | async-done | bytes 2097168
  469.7 1.4 convolution_add_fusion.2
  471.1 1.6 fusion.72
  472.8 1.3 fusion.58
  474.1 1.4 convolution_divide_fusion.1
  475.4 2.3 fusion.115
  477.8 2.3 fusion.117
  480.0 2.3 fusion.119
  482.4 1.3 fusion.57
  483.6 1.3 fusion.56
  484.9 1.3 fusion.55
  486.3 2.0 fusion.62
  488.3 2.0 fusion.65
  490.3 7.9 %fusion.69 = f32[227,512]{1,0:T(8,128)} fusion(f32[4,384,512]{2,1,0:T(8,128)} %get-tuple-element.48, f32[4,512,384]{1,2,0:T(8,128)} %fusion.119, f32[4,512,384]{1,2,0:T(8,128)} %fusion.115, f32[4,512,384]{1,2,0:T(8,128)} %fusion.117, bf16[4,384,512]{2,1,0:T(8,128)(2,1)S(1)} %multiply_convert_fusion, f32[384]{0:T(512)S(1)} %copy-done.28, ...), kind=kOutput, calls=%fused_computation.91 | convolution fusion | flops 1172570112 | bytes 15843840 | tf_op jit(solution)/shard_map/sci,scd->id/dot_general | solution.py:26
  498.9 162.0 %all-reduce.16.cloned.1.call-done = (f32[227,512]{1,0:T(8,128)}, f32[6,512,512]{2,1,0:T(8,128)}, f32[512,83]{0,1:T(8,128)}) async-done(((f32[227,512]{1,0:T(8,128)}, f32[6,512,512]{2,1,0:T(8,128)}, f32[512,83]{0,1:T(8,128)}), (f32[227,512]{1,0:T(8,128)}, f32[6,512,512]{2,1,0:T(8,128)}, f32[512,83]{0,1:T(8,128)})) %all-reduce.16.cloned.1.call-update) | async-done | bytes 6926352 | tf_op jit(solution)/shard_map/psum | solution.py:188
  661.0 5.2 multiply_reduce_fusion.1
  666.2 2.3 multiply_reduce_fusion.3
  668.6 2.1 multiply_reduce_fusion.5
  670.7 2.7 maximum_bitcast_fusion
  673.3 6.8 psum.47
  682.1 1.5 fusion.160
  683.6 3.6 fusion.161
  (116 shorter events, 11.1 us)
Async XLA Ops:
  7.2 3.3 copy-start.13
  7.2 10.4 %copy-start.24 = (s32[384]{0:T(512)S(1)}, s32[384]{0:T(512)}, u32[]{:S(2)}) copy-start(s32[384]{0:T(512)} %param.20) | copy-start | bytes 4612
  7.2 10.5 %copy-start.33 = (bf16[4,384,227]{1,0,2:T(4,128)(2,1)S(1)}, bf16[4,384,227]{1,0,2:T(4,128)(2,1)}, u32[]{:S(2)}) copy-start(bf16[4,384,227]{1,0,2:T(4,128)(2,1)} %param.16) | copy-start | bytes 2092036
  7.2 34.3 %all-gather.5.cloned.1.call-start = ((), (), s32[]{:S(2)}) async-start(), calls=%async_computation | async-start | bytes 3932160 | tf_op jit(solution)/shard_map/all_gather | solution.py:82
  9.8 58.9 %all-gather.9.cloned.1.call-start = ((), (), s32[]{:S(2)}) async-start(), calls=%async_computation.2 | async-start | bytes 2621440 | tf_op jit(solution)/shard_map/all_gather | solution.py:106
  17.6 2.8 copy-start.27
  17.7 2.7 copy-start.37
  20.4 1.1 copy-start.9
  22.0 24.9 %copy-start.39 = (bf16[4,64,512]{2,1,0:T(8,128)(2,1)}, bf16[4,64,512]{2,1,0:T(8,128)(2,1)S(1)}, u32[]{:S(2)}) copy-start(bf16[4,64,512]{2,1,0:T(8,128)(2,1)S(1)} %fusion.73) | copy-start | bytes 786436
  22.0 46.7 %copy-start.23 = (s32[1024]{0:T(1024)S(1)}, s32[1024]{0:T(1024)}, u32[]{:S(2)}) copy-start(s32[1024]{0:T(1024)} %param.22) | copy-start | bytes 12292
  43.7 2.3 copy-start.5
  46.0 74.0 %all-gather.7.cloned.1.call-start = ((), (), s32[]{:S(2)}) async-start(), calls=%async_computation.1 | async-start | bytes 2359296 | tf_op jit(solution)/shard_map/all_gather | solution.py:109
  46.7 178.3 %all-reduce.10.cloned.1.call-start = ((), (), s32[]{:S(2)}) async-start(), calls=%async_computation.4 | async-start | bytes 4194304
  68.7 6.5 copy-start.1
  79.9 43.0 %copy-start.29 = (s32[1024]{0:T(1024)S(1)}, s32[1024]{0:T(1024)}, u32[]{:S(2)}) copy-start(s32[1024]{0:T(1024)} %param.21) | copy-start | bytes 12292
  159.1 6.0 copy-start.3
  171.7 3.3 copy-start.19
  171.7 3.3 copy-start.36
  171.7 10.5 %copy-start.31 = (f32[384]{0:T(512)S(1)}, f32[384]{0:T(512)}, u32[]{:S(2)}) copy-start(f32[384]{0:T(512)} %param.18) | copy-start | bytes 4612
  171.7 54.5 %copy-start.7 = (bf16[6,512,512]{2,1,0:T(8,128)(2,1)S(1)}, bf16[6,512,512]{2,1,0:T(8,128)(2,1)}, u32[]{:S(2)}) copy-start(bf16[6,512,512]{2,1,0:T(8,128)(2,1)} %all-gather.5.cloned.1.call-done) | copy-start | bytes 9437188
  174.9 129.1 %all-gather.11.cloned.1.call-start = ((), (), s32[]{:S(2)}) async-start(), calls=%async_computation.3 | async-start | bytes 1310720 | tf_op jit(solution)/shard_map/all_gather | solution.py:150
  229.2 2.5 copy-start.10
  231.8 4.2 copy-start.20
  234.8 1.1 copy-start.8
  237.2 43.6 %copy-start.15 = (f32[4,384,83]{1,2,0:T(8,128)}, f32[4,384,83]{1,2,0:T(8,128)S(1)}, u32[]{:S(2)}) copy-start(f32[4,384,83]{1,2,0:T(8,128)S(1)} %get-tuple-element.54) | copy-start | bytes 1529860
  286.3 76.0 %all-reduce.14.cloned.1.call-start = ((), (), s32[]{:S(2)}) async-start(), calls=%async_computation.6 | async-start | bytes 2097152
  310.5 12.0 %copy-start = (f32[4,1024,512]{1,2,0:T(8,128)}, f32[4,1024,512]{1,2,0:T(8,128)S(1)}, u32[]{:S(2)}) copy-start(f32[4,1024,512]{1,2,0:T(8,128)S(1)} %fusion) | copy-start | bytes 25165828
  311.9 1.4 copy-start.30
  325.8 142.9 %all-reduce.12.cloned.1.call-start = ((), (), s32[]{:S(2)}) async-start(), calls=%async_computation.5 | async-start | bytes 4194304
  338.5 4.6 copy-start.35
  338.5 5.9 copy-start.16
  343.0 317.9 %all-reduce.16.cloned.1.call-start = ((), (), s32[]{:S(2)}) async-start(), calls=%async_computation.7 | async-start | bytes 13893632 | tf_op jit(solution)/shard_map/psum | solution.py:188
  363.3 109.4 %copy-start.40 = (bf16[4,64,512]{2,1,0:T(8,128)(2,1)S(1)}, bf16[4,64,512]{2,1,0:T(8,128)(2,1)}, u32[]{:S(2)}) copy-start(bf16[4,64,512]{2,1,0:T(8,128)(2,1)} %copy-done.39) | copy-start | bytes 786436
  471.1 2.9 copy-start.38
  477.8 4.6 copy-start.6
  482.4 3.9 copy-start.12
  486.3 2.0 copy-start.11
  488.3 2.0 copy-start.28
  488.3 2.0 copy-start.34
  498.1 162.8 %copy-start.2 = (f32[6,128,512]{2,1,0:T(8,128)S(1)}, f32[6,128,512]{2,1,0:T(8,128)}, u32[]{:S(2)}) copy-start(f32[6,128,512]{2,1,0:T(8,128)} %param.24) | copy-start | bytes 4718596
  660.9 5.2 copy-start.14
  661.0 5.2 copy-start.21
  661.0 5.2 copy-start.22
  661.0 7.6 %copy-start.25 = (f32[128,83]{0,1:T(8,128)S(1)}, f32[128,83]{0,1:T(8,128)}, u32[]{:S(2)}) copy-start(f32[128,83]{0,1:T(8,128)} %param.31) | copy-start | bytes 127492
  661.0 7.6 %copy-start.26 = (f32[128,83]{0,1:T(8,128)S(1)}, f32[128,83]{0,1:T(8,128)}, u32[]{:S(2)}) copy-start(f32[128,83]{0,1:T(8,128)} %param.28) | copy-start | bytes 127492
  666.2 21.0 %copy-start.4 = (f32[6,128,512]{2,1,0:T(8,128)}, f32[6,128,512]{2,1,0:T(8,128)S(1)}, u32[]{:S(2)}) copy-start(f32[6,128,512]{2,1,0:T(8,128)S(1)} %get-tuple-element.37) | copy-start | bytes 4718596
  668.5 18.7 %copy-start.17 = (f32[227,128]{1,0:T(8,128)}, f32[227,128]{1,0:T(8,128)S(1)}, u32[]{:S(2)}) copy-start(f32[227,128]{1,0:T(8,128)S(1)} %get-tuple-element.34) | copy-start | bytes 348676
  668.5 18.7 %copy-start.18 = (f32[227,128]{1,0:T(8,128)}, f32[227,128]{1,0:T(8,128)S(1)}, u32[]{:S(2)}) copy-start(f32[227,128]{1,0:T(8,128)S(1)} %get-tuple-element.35) | copy-start | bytes 348676
  680.2 7.0 %copy-start.32 = (f32[2,8]{1,0:T(2,128)}, f32[2,8]{1,0:T(2,128)S(1)}, u32[]{:S(2)}) copy-start(f32[2,8]{1,0:T(2,128)S(1)} %sqrt.15) | copy-start | bytes 196
Sparse Core Ops, SparseCore 0:
  10.2 31.3 all-gather.4
  46.1 22.5 all-gather.8
  70.9 49.0 all-gather.6
  175.1 49.9 all-reduce.9
  286.4 17.5 all-gather.10
  325.9 36.2 all-reduce.13
  365.9 102.7 all-reduce.11
  498.3 162.6 all-reduce.15
where the time goes:
time: 700 us; the launch traced here: 696 us
  waiting for transfers between devices  425 us (61%)
  matrix products  152 us (22%)
  blocking collectives  59.5 us (8%)
  other arithmetic  22.6 us (3%)
  between operations  20.6 us (3%)
  local copies, waits for them, and re-layouts  15.9 us (2%)
    unnamed x11, waiting for transfers between devices  164 us
    psum x1, waiting for transfers between devices, body(): lax.psum((local_terms[0], local_terms[1], local_terms[2]), ('row', 'col'))  162 us
    dot_general x42, matrix products, reduced_matmul(): return jnp.einsum(form, left, right, preferred_element_type=jnp.float32)  151 us
    all_gather x1, waiting for transfers between devices, body(): lax.all_gather(mesh_state_reduced, 'row', axis=1, tiled=True)  40 us
    psum x1, blocking collectives, body(): lax.psum(jnp.sum(weighted * error), ('row', 'col')) / denominator  39.6 us
    all_gather x1, waiting for transfers between devices, body(): lax.all_gather(receiver_local_part, 'col', axis=1, tiled=True)  21.7 us
    all_gather x1, waiting for transfers between devices, body(): lax.all_gather(weight_latent.astype(jnp.bfloat16), 'col', axis=1, tiled=T...  19.5 us
    all_gather x1, waiting for transfers between devices, body(): d_block = lax.all_gather(message_total_gradient, 'col', axis=1, tiled=True)  17.5 us
  transfers between devices with their start and end apart: 8, of which 8 were waited for; matrix products, arithmetic and copies ran while one was open for 5% of the time, Pallas kernels for 0%

commit v1 on v0

--- a/solution.py
+++ b/solution.py
@@ -1,6 +1,11 @@
+import functools
+import types
+
 import jax
 import jax.numpy as jnp
 from jax import lax
+from jax.experimental import pallas as pl
+from jax.experimental.pallas import tpu as pltpu
 from jax.sharding import PartitionSpec as P
 
 C_OUT = 83
@@ -59,7 +64,856 @@
     return (new_first, new_second, update)
 
 
-def body(
+MESH = pl.DeviceIdType.MESH
+bf16 = jnp.bfloat16
+f32 = jnp.float32
+VMEM_ROOM = 63 * 2**20
+N_IN = 256
+N_OUT = 128
+WIRE = ("in", 0, 1, 2, 5, 3, 4, "out")
+
+
+def sizes_of(n_row, n_col):
+    X = n_col // 2
+    Y = X if n_row % X == 0 else 1
+    return X, Y, n_row // Y
+
+
+class Place:
+    def __init__(self, n_row, n_col):
+        self.K = 2
+        self.X, self.Y, self.Z = sizes_of(n_row, n_col)
+        self.row, self.col = lax.axis_index("row"), lax.axis_index("col")
+        self.z, self.y = self.row // self.Y, self.row % self.Y
+        self.x, self.k = self.col // 2, self.col % 2
+
+    def to(self, axis, d):
+        n = getattr(self, axis.upper())
+        return (getattr(self, axis) + d) % n
+
+    def peer(self, axis, d):
+        at = {a: getattr(self, a) for a in "zyxk"}
+        at[axis] = self.to(axis, d)
+        return (at["z"] * self.Y + at["y"], at["x"] * 2 + at["k"])
+
+    def barrier(self):
+        sem = pltpu.get_barrier_semaphore()
+        peers = [self.peer(a, d) for a in "kxyz" for d in range(1, getattr(self, a.upper()))]
+        for peer in peers:
+            pl.semaphore_signal(sem, inc=1, device_id=peer, device_id_type=MESH)
+        pl.semaphore_wait(sem, len(peers))
+
+
+def remote(src, dst, send_sem, recv_sem, device):
+    return pltpu.make_async_remote_copy(
+        src_ref=src,
+        dst_ref=dst,
+        send_sem=send_sem,
+        recv_sem=recv_sem,
+        device_id=device,
+        device_id_type=MESH,
+    )
+
+
+def ds(start, size):
+    if isinstance(start, int):
+        return pl.ds(start, size)
+    return pl.ds(pl.multiple_of(start, size if size % 128 else 128), size)
+
+
+def by_rows(count, step, todo):
+    def one(i, carry):
+        todo(pl.multiple_of(i * step, step))
+        return carry
+
+    lax.fori_loop(0, count // step, one, 0)
+
+
+def mm(a, b):
+    return jnp.dot(a, b, preferred_element_type=f32)
+
+
+def mm_nt(a, b):
+    return lax.dot_general(a, b, (((1,), (1,)), ((), ())), preferred_element_type=f32)
+
+
+def mm_tn(a, b):
+    return lax.dot_general(a, b, (((0,), (0,)), ((), ())), preferred_element_type=f32)
+
+
+def sigmoid(v):
+    return 0.5 * jnp.tanh(0.5 * v) + 0.5
+
+
+def silu(v):
+    return v * sigmoid(v)
+
+
+def silu_slope(v):
+    s = sigmoid(v)
+    return s * (1.0 + v * (1.0 - s))
+
+
+def high_low(v):
+    high = v.astype(bf16)
+    return high, (v - high.astype(f32)).astype(bf16)
+
+
+class Total:
+    AXES = "kxyz"
+
+    @staticmethod
+    def scratch(X, Y, Z):
+        many = 1 + X - 1 + Y - 1 + Z - 1
+        return [pltpu.VMEM((n, 8, 128), f32) for n in (2, X, Y, Z)] + [
+            pltpu.VMEM((8, 128), f32),
+            pltpu.SemaphoreType.DMA((many,)),
+            pltpu.SemaphoreType.DMA((many,)),
+        ]
+
+    def __init__(self, place, refs):
+        self.p, self.bufs, (self.value, self.ss, self.rs) = place, dict(zip("kxyz", refs[:4])), refs[4:]
+
+    def _copies(self, axis):
+        p, buf = self.p, self.bufs[axis]
+        base = sum(getattr(p, a.upper()) - 1 for a in self.AXES[: self.AXES.index(axis)])
+        here = buf.at[getattr(p, axis)]
+        for d in range(1, getattr(p, axis.upper())):
+            i = base + d - 1
+            yield remote(here, here, self.ss.at[i], self.rs.at[i], p.peer(axis, d))
+
+    def start(self, axis):
+        self.bufs[axis][getattr(self.p, axis)] = self.value[...]
+        for copy in self._copies(axis):
+            copy.start()
+
+    def finish(self, axis):
+        for copy in self._copies(axis):
+            copy.wait_recv()
+        buf = self.bufs[axis]
+        value = buf[0]
+        for i in range(1, getattr(self.p, axis.upper())):
+            value = value + buf[i]
+        self.value[...] = value
+
+    def drain(self):
+        for axis in self.AXES:
+            for copy in self._copies(axis):
+                copy.wait_send()
+
+
+class Reduce:
+    def __init__(self, grid, dim, n_col, width, late):
+        self.X, self.Y, self.Z = grid
+        self.dim, self.shard, self.late = dim, dim // n_col, late
+        self.ry = self.shard // self.Y
+        self.zr = min(self.ry // 16, self.Z)
+        self.zl = self.Z // self.zr
+        self.rz = self.ry // self.zr
+        self.w = -(-width // (128 * self.zl)) * 128 * self.zl
+        self.wz = self.w // self.zl
+
+    def scratch(self):
+        X, Y, Z, w = self.X, self.Y, self.Z, self.w
+        many = X + (X - 1) + 2 * (Y - 1) + 2 * (Z - 1)
+        return [
+            pltpu.VMEM((self.dim, w), f32),
+            pltpu.VMEM((X, self.shard, w), f32),
+            pltpu.VMEM((X - 1, self.shard, w), bf16),
+            pltpu.VMEM((X - 1, self.shard, w), bf16),
+            pltpu.VMEM((Y - 1, self.ry, w), bf16),
+            pltpu.VMEM((Y - 1, self.ry, w), bf16),
+            pltpu.VMEM((Z - 1, self.rz, self.wz), self.late),
+            pltpu.VMEM((Z - 1, self.rz, self.wz), self.late),
+            pltpu.VMEM((self.rz, self.wz), f32),
+            pltpu.VMEM((self.shard, w), self.late),
+            pltpu.SemaphoreType.DMA((many,)),
+            pltpu.SemaphoreType.DMA((many,)),
+        ]
+
+    def bind(self, place, refs):
+        (self.full, self.cr, self.xs, self.xr, self.ys, self.yr, self.zs, self.zin, self.piece, self.out, self.ss, self.rs) = refs
+        self.p = place
+        self.copies = []
+
+    def rows_of(self, x, k):
+        return (2 * x + k) * self.shard
+
+    def piece_at(self, z):
+        rows = pl.multiple_of((z // self.zl) * self.rz, 16)
+        if self.zl == 1:
+            return rows, pl.ds(0, self.wz)
+        return rows, pl.ds(pl.multiple_of((z % self.zl) * self.wz, 128), self.wz)
+
+    def _send(self, i, src, dst, device):
+        copy = remote(src, dst, self.ss.at[i], self.rs.at[i], device)
+        copy.start()
+        self.copies.append(copy)
+        return copy
+
+    def stage(self, s):
+        p, X, Y, Z = self.p, self.X, self.Y, self.Z
+        if s == 0:
+            self.core = [
+                self._send(x, self.full.at[ds(self.rows_of(x, 1 - p.k), self.shard), :], self.cr.at[x], p.peer("k", 1))
+                for x in range(X)
+            ]
+        elif s == 1:
+            for copy in self.core:
+                copy.wait_recv()
+            self.xc = []
+            for d in range(1, X):
+                to = p.to("x", d)
+
+                def one(at, to=to, d=d):
+                    mine = self.full[pl.ds(pl.multiple_of(self.rows_of(to, p.k) + at, 16), 16), :]
+                    self.xs[d - 1, pl.ds(at, 16), :] = (mine + self.cr[to, pl.ds(at, 16), :]).astype(bf16)
+
+                by_rows(self.shard, 16, one)
+                self.xc.append(self._send(X + d - 1, self.xs.at[d - 1], self.xr.at[d - 1], p.peer("x", d)))
+        elif s == 2:
+            for copy in self.xc:
+                copy.wait_recv()
+
+            def total(at, n=16):
+                value = self.full[pl.ds(pl.multiple_of(self.rows_of(p.x, p.k) + at, 16), n), :]
+                value = value + self.cr[p.x, pl.ds(at, n), :]
+                for d in range(1, X):
+                    value = value + self.xr[d - 1, pl.ds(at, n), :].astype(f32)
+                return value
+
+            self.yc = []
+            for d in range(1, Y):
+                base = p.to("y", d) * self.ry
+
+                def one(at, base=base, d=d):
+                    self.ys[d - 1, pl.ds(at, 16), :] = total(pl.multiple_of(base + at, 16)).astype(bf16)
+
+                by_rows(self.ry, 16, one)
+                self.yc.append(self._send(2 * X - 2 + d, self.ys.at[d - 1], self.yr.at[d - 1], p.peer("y", d)))
+
+            def mine(at):
+                at = pl.multiple_of(p.y * self.ry + at, 16)
+                self.cr[p.x, pl.ds(at, 16), :] = total(at)
+
+            by_rows(self.ry, 16, mine)
+        elif s == 3:
+            for copy in self.yc:
+                copy.wait_recv()
+
+            def total(z):
+                rows, lanes = self.piece_at(z)
+                value = self.cr[p.x, pl.ds(pl.multiple_of(p.y * self.ry + rows, 16), self.rz), lanes]
+                for d in range(1, Y):
+                    value = value + self.yr[d - 1, pl.ds(rows, self.rz), lanes].astype(f32)
+                return value
+
+            self.zc = []
+            base = 2 * X - 1 + Y - 1
+            for d in range(1, Z):
+                self.zs[d - 1] = total(p.to("z", d)).astype(self.late)
+                self.zc.append(self._send(base + d - 1, self.zs.at[d - 1], self.zin.at[d - 1], p.peer("z", d)))
+            self.piece[...] = total(p.z)
+        elif s == 4:
+            for copy in self.zc:
+                copy.wait_recv()
+            value = self.piece[...]
+            for d in range(1, Z):
+                value = value + self.zin[d - 1].astype(f32)
+            self.piece[...] = value
+            rows, lanes = self.piece_at(p.z)
+            here = self.out.at[pl.ds(pl.multiple_of(p.y * self.ry + rows, 16), self.rz), lanes]
+            here[...] = value.astype(self.late)
+            base = 2 * X - 1 + Y - 1 + Z - 1
+            self.gz = [self._send(base + d - 1, here, here, p.peer("z", d)) for d in range(1, Z)]
+        elif s == 5:
+            for copy in self.gz:
+                copy.wait_recv()
+            here = self.out.at[pl.ds(pl.multiple_of(p.y * self.ry, 16), self.ry), :]
+            base = 2 * X - 1 + Y - 1 + 2 * (Z - 1)
+            self.gy = [self._send(base + d - 1, here, here, p.peer("y", d)) for d in range(1, Y)]
+        elif s == 6:
+            for copy in self.gy:
+                copy.wait_recv()
+
+    def drain(self):
+        for copy in self.copies:
+            copy.wait_send()
+
+
+STAGES = 7
+
+
+class Step:
+    def __init__(self, mesh, samples, slots, dim, edges, c_in):
+        self.n_row, self.n_col = mesh.shape["row"], mesh.shape["col"]
+        self.grid = sizes_of(self.n_row, self.n_col)
+        self.S, self.C, self.D, self.E, self.c_in = samples, slots, dim, edges, c_in
+        self.N = MESH_DEV
+        self.SH = dim // self.n_col
+        self.R, self.Q = self.n_row * self.N, self.n_col * self.N
+        chunk = lambda width, late: Reduce(self.grid, dim, self.n_col, width, late)
+        self.chunks = [
+            chunk(dim + N_OUT, f32),
+            chunk(2 * dim, bf16),
+            chunk(2 * dim, bf16),
+            chunk(dim, bf16),
+            chunk(N_IN, f32),
+        ]
+        X, Y, Z = self.grid
+        S, C, D, E, N, R, Q = self.S, self.C, self.D, self.E, self.N, self.R, self.Q
+        vm = pltpu.VMEM
+        dma = lambda *shape: pltpu.SemaphoreType.DMA(shape)
+        self.shapes = dict(
+            wib=vm((D, N_IN), bf16),
+            wlb=vm((6, D, D), bf16),
+            wob=vm((D, N_OUT), bf16),
+            nm=vm((N, C), bf16),
+            nv=vm((N, C), bf16),
+            cm=vm((C, N), bf16),
+            cmv=vm((C, N), bf16),
+            cw=vm((C, 128), f32),
+            cnt=vm((N, 128), f32),
+            fp=vm((S * C, D), f32),
+            gl=vm((S * C, D), bf16),
+            tp=vm((S * C, D), f32),
+            go=vm((S * C, D), bf16),
+            dp=vm((S * C, N_OUT), bf16),
+            dt=vm((S * C, D), bf16),
+            av=vm((S * N, D), bf16),
+            sp=vm((S * N, D), f32),
+            ml=vm((S * N, D), f32),
+            mlb=vm((S * N, D), bf16),
+            agb=vm((S * N, D), bf16),
+            mnb=vm((S * N, D), bf16),
+            sg=vm((S * N, D), f32),
+            dmn=vm((S * N, D), f32),
+            dbb=vm((S * N, D), bf16),
+            dsb=vm((S * N, D), bf16),
+            drb=vm((S * N, D), bf16),
+            d2b=vm((S * N, D), bf16),
+            sr=vm((S, R + Q, D), bf16),
+            oh=vm((E, R + Q), bf16),
+            oht=vm((R + Q, E), bf16),
+            ep=vm((S, E, D), f32),
+            ac=vm((E, D), bf16),
+            tmp=vm((R + Q, D), f32),
+            part=vm((S, Q, D), f32),
+            pcr=vm((S, X, N, D), f32),
+            pxs=vm((S, X - 1, N, D), bf16),
+            pxr=vm((S, X - 1, N, D), bf16),
+            da=vm((S, Q, D), bf16),
+            down=vm((S, Z, N, D), f32),
+            dys=vm((S, Y - 1, Z, N, D), bf16),
+            dyr=vm((S, Y - 1, Z, N, D), bf16),
+            dzs=vm((S, Z - 1, N, D), bf16),
+            dzr=vm((S, Z - 1, N, D), bf16),
+            loss=vm((8, 128), f32),
+            l_sem=dma(6),
+            w_ss=dma(8, 1 + 2 * (X - 1)),
+            w_rs=dma(8, 1 + 2 * (X - 1)),
+            mz_ss=dma(S, Z - 1),
+            mz_rs=dma(S, Z - 1),
+            my_ss=dma(S, Y - 1, Z),
+            my_rs=dma(S, Y - 1, Z),
+            mr_ss=dma(S, 1 + 2 * (X - 1)),
+            mr_rs=dma(S, 1 + 2 * (X - 1)),
+            pk_ss=dma(2, S, X),
+            pk_rs=dma(2, S, X),
+            px_ss=dma(2, S, X - 1),
+            px_rs=dma(2, S, X - 1),
+            a_ss=dma(S, 1 + 2 * (X - 1)),
+            a_rs=dma(S, 1 + 2 * (X - 1)),
+            dy_ss=dma(S, Y - 1),
+            dy_rs=dma(S, Y - 1),
+            dz_ss=dma(S, Z - 1),
+            dz_rs=dma(S, Z - 1),
+        )
+
+    def vmem_bytes(self):
+        total = 0
+        for s in [*self.shapes.values(), *[s for c in self.chunks for s in c.scratch()]]:
+            dtype = getattr(s, "dtype", None)
+            if dtype in (jnp.dtype(f32), jnp.dtype(bf16)):
+                size = jnp.dtype(dtype).itemsize
+                for n in s.shape[:-1]:
+                    size *= n
+                total += size * -(-s.shape[-1] // 128) * 128
+        return total
+
+    def scratch(self):
+        total = Total.scratch(*self.grid)
+        return [*self.shapes.values(), *total, *total, *[s for c in self.chunks for s in c.scratch()]]
+
+    def kernel(self, count, x, tgt, area, node, snd, rcv, wit, wl, wo, *refs):
+        S, C, D, E, N, R, Q, SH = self.S, self.C, self.D, self.E, self.N, self.R, self.Q, self.SH
+        X, Y, Z = self.grid
+        outs, stats, refs = refs[:5], refs[5], refs[6:]
+        v = types.SimpleNamespace(**dict(zip(self.shapes, refs)))
+        refs = refs[len(self.shapes) :]
+        p = Place(self.n_row, self.n_col)
+        area_sum, loss_sum = Total(p, refs[:7]), Total(p, refs[7:14])
+        refs = refs[14:]
+        for chunk in self.chunks:
+            many = len(chunk.scratch())
+            chunk.bind(p, refs[:many])
+            refs = refs[many:]
+
+        def weight_rows(i, col):
+            which = WIRE[i]
+            whole = v.wib if which == "in" else v.wob if which == "out" else v.wlb.at[which]
+            return whole.at[ds(col * SH, SH), :]
+
+        def w_copy(i, j, d=0):
+            rows = weight_rows(i, 2 * p.to("x", -d) + p.k if j == 2 else p.col)
+            at = (0, d, X - 1 + d)[j]
+            device = p.peer("x", d) if j == 1 else p.peer("k", 1)
+            return remote(rows, rows, v.w_ss.at[i, at], v.w_rs.at[i, at], device)
+
+        hops = range(1, X)
+
+        def w_forward(i):
+            for d in hops:
+                w_copy(i, 1, d).wait_recv()
+                w_copy(i, 2, d).start()
+
+        def w_get(i):
+            w_copy(i, 0).wait_recv()
+            for d in hops:
+                w_copy(i, 2, d).wait_recv()
+
+        W = lambda which: v.wlb[which]
+        own = ds(p.col * SH, SH)
+        v.wib[own, :] = wit[...]
+        loads = [pltpu.make_async_copy(wl.at[m], v.fp.at[m * SH : (m + 1) * SH, :], v.l_sem.at[m]) for m in range(6)]
+        for load in loads:
+            load.start()
+        for m, load in enumerate(loads):
+            load.wait()
+            v.wlb[m, own, :] = v.fp[m * SH : (m + 1) * SH, :].astype(bf16)
+        v.wob[own, :] = jnp.zeros((SH, N_OUT), bf16)
+        v.wob[own, 0:C_OUT] = wo[...].astype(bf16)
+        p.barrier()
+        for i in range(8):
+            w_copy(i, 0).start()
+            for d in hops:
+                w_copy(i, 1, d).start()
+
+        used = count[0]
+        node_row = node[...]
+        match = (lax.broadcasted_iota(jnp.int32, (N, C), 0) == node_row).astype(f32)
+        v.nm[...] = match.astype(bf16)
+        match = match * (lax.broadcasted_iota(jnp.int32, (N, C), 1) < used).astype(f32)
+        v.nv[...] = match.astype(bf16)
+        v.cnt[...] = jnp.broadcast_to(jnp.maximum(jnp.sum(match, axis=1, keepdims=True), 1.0), (N, 128))
+        node_col = jnp.transpose(jnp.broadcast_to(node_row, (128, C)))
+        area_row = area[...] * (lax.broadcasted_iota(jnp.int32, (1, C), 1) < used).astype(f32)
+        v.cw[...] = jnp.transpose(jnp.broadcast_to(area_row, (128, C)))
+        match = (lax.broadcasted_iota(jnp.int32, (C, 128), 1) == node_col).astype(f32)
+        v.cm[...] = match[:, :N].astype(bf16)
+        match = match * (lax.broadcasted_iota(jnp.int32, (C, 128), 0) < used).astype(f32)
+        v.cmv[...] = match[:, :N].astype(bf16)
+        area_sum.value[...] = jnp.broadcast_to(jnp.sum(area_row), (8, 128))
+        area_sum.start("k")
+
+        w_forward(0)
+        w_get(0)
+
+        def encode(s, carry):
+            at = ds(s * C, C)
+            pre = mm_nt(x[s], v.wib[:, : self.c_in])
+            v.fp[at, :] = pre
+            v.gl[at, :] = silu(pre).astype(bf16)
+            here = ds(s * N, N)
+            v.av[here, :] = (mm(v.nv[...], v.gl[at, :]) / v.cnt[:, 0:1]).astype(bf16)
+            return carry
+
+        lax.fori_loop(0, S, encode, 0)
+        area_sum.finish("k")
+        area_sum.start("x")
+        w_forward(1)
+        w_get(1)
+        pre = mm(v.av[...], W(0))
+        v.sp[...] = pre
+        v.ml[...] = silu(pre)
+        v.mlb[...] = v.ml[...].astype(bf16)
+        w_forward(2)
+        w_get(2)
+        v.tmp[0 : S * N, :] = mm(v.mlb[...], W(1))
+        for s in range(S):
+            v.sr[s, ds(p.row * N, N), :] = v.tmp[s * N : (s + 1) * N, :].astype(bf16)
+        w_forward(3)
+        w_get(3)
+
+        def mz(s, d):
+            rows = v.sr.at[s, ds(p.row * N, N), :]
+            return remote(rows, rows, v.mz_ss.at[s, d - 1], v.mz_rs.at[s, d - 1], p.peer("z", d))
+
+        def my(s, d, e):
+            rows = v.sr.at[s, ds((p.to("z", -e) * Y + p.y) * N, N), :]
+            return remote(rows, rows, v.my_ss.at[s, d - 1, e], v.my_rs.at[s, d - 1, e], p.peer("y", d))
+
+        def mr(s, j, d=0):
+            col = 2 * p.to("x", -d) + p.k if j == 2 else p.col
+            rows = v.sr.at[s, ds(R + col * N, N), :]
+            at = (0, d, X - 1 + d)[j]
+            return remote(rows, rows, v.mr_ss.at[s, at], v.mr_rs.at[s, at], p.peer("x", d) if j == 1 else p.peer("k", 1))
+
+        for s in range(S):
+            for d in range(1, Z):
+                mz(s, d).start()
+            for d in range(1, Y):
+                my(s, d, 0).start()
+        v.tmp[0 : S * N, :] = mm(v.mlb[...], W(2))
+        for s in range(S):
+            v.sr[s, ds(R + p.col * N, N), :] = v.tmp[s * N : (s + 1) * N, :].astype(bf16)
+        for s in range(S):
+            mr(s, 0).start()
+            for d in hops:
+                mr(s, 1, d).start()
+        area_sum.finish("x")
+        area_sum.start("y")
+
+        def table(index, base, rows):
+            def down(at):
+                hit = lax.broadcasted_iota(jnp.int32, (128, E), 0) + at == index
+                v.oht[pl.ds(pl.multiple_of(base + at, 128), 128), :] = hit.astype(f32).astype(bf16)
+
+            by_rows(rows, 128, down)
+            column = jnp.transpose(jnp.broadcast_to(index, (128, E)))
+            for at in range(0, rows, 128):
+                hit = lax.broadcasted_iota(jnp.int32, (E, 128), 1) + at == column
+                v.oh[:, base + at : base + at + 128] = hit.astype(f32).astype(bf16)
+
+        table(snd[...], 0, R)
+        table(rcv[...], R, Q)
+
+        w_forward(4)
+        w_get(4)
+
+        def skip(at):
+            v.tp[pl.ds(at, 512), :] = mm(v.gl[pl.ds(at, 512), :], W(5))
+
+        by_rows(S * C, 512, skip)
+        area_sum.finish("y")
+        area_sum.start("z")
+        w_forward(5)
+
+        def pk(t, s, xx):
+            rows = v.part.at[s, ds((2 * xx + 1 - p.k) * N, N), :]
+            return remote(rows, v.pcr.at[s, xx], v.pk_ss.at[t, s, xx], v.pk_rs.at[t, s, xx], p.peer("k", 1))
+
+        def px(t, s, d):
+            return remote(v.pxs.at[s, d - 1], v.pxr.at[s, d - 1], v.px_ss.at[t, s, d - 1], v.px_rs.at[t, s, d - 1], p.peer("x", d))
+
+        def col_second(t, s):
+            for xx in range(X):
+                pk(t, s, xx).wait_recv()
+            for d in hops:
+                px_to = p.to("x", d)
+                mine = v.part[s, ds((2 * px_to + p.k) * N, N), :]
+                v.pxs[s, d - 1] = (mine + v.pcr[s, px_to]).astype(bf16)
+                px(t, s, d).start()
+
+        def col_last(t, s):
+            total = v.part[s, ds(p.col * N, N), :] + v.pcr[s, p.x]
+            for d in hops:
+                px(t, s, d).wait_recv()
+                total = total + v.pxr[s, d - 1].astype(f32)
+            return total
+
+        def arrive(s):
+            for d in range(1, Z):
+                mz(s, d).wait_recv()
+                for b in range(1, Y):
+                    my(s, b, d).start()
+            for d in hops:
+                mr(s, 1, d).wait_recv()
+                mr(s, 2, d).start()
+
+        def edges(s):
+            for b in range(1, Y):
+                for e in range(Z):
+                    my(s, b, e).wait_recv()
+            mr(s, 0).wait_recv()
+            for d in hops:
+                mr(s, 2, d).wait_recv()
+
+            def pick(at):
+                pre = mm(v.oh[pl.ds(at, 512), :], v.sr[s])
+                v.ep[s, pl.ds(at, 512), :] = pre
+                v.ac[pl.ds(at, 512), :] = silu(pre).astype(bf16)
+
+            by_rows(E, 512, pick)
+            v.part[s] = mm(v.oht[R:, :], v.ac[...])
+            for xx in range(X):
+                pk(0, s, xx).start()
+
+        def forward(i, carry):
+            @pl.when(i < S)
+            def _():
+                arrive(i)
+
+            @pl.when((i >= 1) & (i <= S))
+            def _():
+                edges(i - 1)
+
+            @pl.when(i >= 2)
+            def _():
+                col_second(0, i - 2)
+
+            return carry
+
+        lax.fori_loop(0, S + 2, forward, 0)
+        area_sum.finish("z")
+        w_get(5)
+        for i in (6, 7):
+            w_forward(i)
+        for s in range(S):
+            v.agb[s * N : (s + 1) * N, :] = (col_last(0, s) * (1.0 / DEG)).astype(bf16)
+
+        v.mnb[...] = (v.ml[...] + mm(v.agb[...], W(3))).astype(bf16)
+        w_get(6)
+        w_get(7)
+        v.dp[...] = jnp.zeros((S * C, N_OUT), bf16)
+        v.loss[...] = jnp.zeros((8, 128), f32)
+        scale = 1.0 / (C_OUT * S * area_sum.value[0:1, 0:1])
+
+        def decode(s, carry):
+            at, here = ds(s * C, C), ds(s * N, N)
+            rows = mm(v.cm[...], v.mnb[here, :]).astype(bf16)
+            pre = mm(rows, W(4)) + v.tp[at, :]
+            v.tp[at, :] = pre
+            v.go[at, :] = silu(pre).astype(bf16)
+            error = mm(v.go[at, :], v.wob[...])[:, :C_OUT] - tgt[s].astype(f32)
+            weighted = v.cw[:, :C_OUT] * error
+            v.loss[0:1, 0:C_OUT] = v.loss[0:1, 0:C_OUT] + jnp.sum(weighted * error, axis=0, keepdims=True)
+            v.dp[at, 0:C_OUT] = (2.0 * weighted * scale).astype(bf16)
+            v.dt[at, :] = (silu_slope(v.tp[at, :]) * mm_nt(v.dp[at, :], v.wob[...])).astype(bf16)
+            v.sg[here, :] = mm(v.nm[...], v.dt[at, :])
+            return carry
+
+        lax.fori_loop(0, S, decode, 0)
+        high, low = high_low(v.sg[...])
+        v.dmn[...] = mm_nt(high, W(4)) + mm_nt(low, W(4))
+        v.dbb[...] = v.dmn[...].astype(bf16)
+        v.tmp[0 : S * N, :] = mm_nt(v.dbb[...], W(3))
+        for s in range(S):
+            v.da[s, ds(p.col * N, N), :] = v.tmp[s * N : (s + 1) * N, :].astype(bf16)
+
+        def ac(s, j, d=0):
+            col = 2 * p.to("x", -d) + p.k if j == 2 else p.col
+            rows = v.da.at[s, ds(col * N, N), :]
+            at = (0, d, X - 1 + d)[j]
+            return remote(rows, rows, v.a_ss.at[s, at], v.a_rs.at[s, at], p.peer("x", d) if j == 1 else p.peer("k", 1))
+
+        for s in range(S):
+            ac(s, 0).start()
+            for d in hops:
+                ac(s, 1, d).start()
+        loss_sum.value[...] = jnp.broadcast_to(jnp.sum(v.loss[...]), (8, 128))
+        loss_sum.start("k")
+
+        first, second, third, fourth, fifth = self.chunks
+        first.full[:, 0:D] = mm_tn(v.gl[...], v.dt[...])
+        first.full[:, D : D + N_OUT] = mm_tn(v.go[...], v.dp[...])
+        first.stage(0)
+        high, low = high_low(v.sg[...])
+        second.full[:, 0:D] = mm_tn(v.mnb[...], high) + mm_tn(v.mnb[...], low)
+        second.full[:, D : 2 * D] = mm_tn(v.agb[...], v.dbb[...])
+        second.stage(0)
+
+        def skip_back(at):
+            v.tp[pl.ds(at, 512), :] = mm_nt(v.dt[pl.ds(at, 512), :], W(5))
+
+        by_rows(S * C, 512, skip_back)
+        loss_sum.finish("k")
+        loss_sum.start("x")
+        first.stage(1)
+        second.stage(1)
+
+        def dy(s, d):
+            return remote(v.dys.at[s, d - 1], v.dyr.at[s, d - 1], v.dy_ss.at[s, d - 1], v.dy_rs.at[s, d - 1], p.peer("y", d))
+
+        def dz(s, d):
+            return remote(v.dzs.at[s, d - 1], v.dzr.at[s, d - 1], v.dz_ss.at[s, d - 1], v.dz_rs.at[s, d - 1], p.peer("z", d))
+
+        def pass_on(s):
+            for d in hops:
+                ac(s, 1, d).wait_recv()
+                ac(s, 2, d).start()
+
+        def edges_back(s):
+            ac(s, 0).wait_recv()
+            for d in hops:
+                ac(s, 2, d).wait_recv()
+
+            def pick(at):
+                grad = mm(v.oh[pl.ds(at, 512), R:], v.da[s])
+                v.ac[pl.ds(at, 512), :] = (silu_slope(v.ep[s, pl.ds(at, 512), :]) * grad * (1.0 / DEG)).astype(bf16)
+
+            by_rows(E, 512, pick)
+            v.tmp[...] = mm(v.oht[...], v.ac[...])
+            for d in range(1, Y):
+                for e in range(Z):
+                    v.dys[s, d - 1, e] = v.tmp[ds((e * Y + p.to("y", d)) * N, N), :].astype(bf16)
+                dy(s, d).start()
+            for e in range(Z):
+                v.down[s, e] = v.tmp[ds((e * Y + p.y) * N, N), :]
+            v.part[s] = v.tmp[R:, :]
+            for xx in range(X):
+                pk(1, s, xx).start()
+
+        def row_second(s):
+            for d in range(1, Y):
+                dy(s, d).wait_recv()
+
+            def summed(e):
+                total = v.down[s, e]
+                for d in range(1, Y):
+                    total = total + v.dyr[s, d - 1, e].astype(f32)
+                return total
+
+            for d in range(1, Z):
+                v.dzs[s, d - 1] = summed(p.to("z", d)).astype(bf16)
+                dz(s, d).start()
+            v.down[s, p.z] = summed(p.z)
+
+        for s in range(S):
+            for xx in range(X):
+                pk(0, s, xx).wait_send()
+            for d in hops:
+                px(0, s, d).wait_send()
+
+        def backward(i, carry):
+            @pl.when(i < S)
+            def _():
+                pass_on(i)
+                edges_back(i)
+
+            @pl.when(i >= 1)
+            def _():
+                col_second(1, i - 1)
+                row_second(i - 1)
+
+            return carry
+
+        lax.fori_loop(0, S + 1, backward, 0)
+        first.stage(2)
+        second.stage(2)
+        for s in range(S):
+            v.drb[s * N : (s + 1) * N, :] = col_last(1, s).astype(bf16)
+        for s in range(S):
+            total = v.down[s, p.z]
+            for d in range(1, Z):
+                dz(s, d).wait_recv()
+                total = total + v.dzr[s, d - 1].astype(f32)
+            v.dsb[s * N : (s + 1) * N, :] = total.astype(bf16)
+
+        third.full[:, 0:D] = mm_tn(v.mlb[...], v.dsb[...])
+        third.full[:, D : 2 * D] = mm_tn(v.mlb[...], v.drb[...])
+        third.stage(0)
+        whole = v.dmn[...] + mm_nt(v.dsb[...], W(1)) + mm_nt(v.drb[...], W(2))
+        v.d2b[...] = (silu_slope(v.sp[...]) * whole).astype(bf16)
+        third.stage(1)
+        fourth.full[...] = mm_tn(v.av[...], v.d2b[...])
+        fourth.stage(0)
+        v.dmn[...] = mm_nt(v.d2b[...], W(0))
+        first.stage(3)
+        second.stage(3)
+
+        def encode_back(s, carry):
+            at, here = ds(s * C, C), ds(s * N, N)
+            high, low = high_low(v.dmn[here, :] / v.cnt[:, 0:1])
+            grad = v.tp[at, :] + mm(v.cmv[...], high) + mm(v.cmv[...], low)
+            v.dt[at, :] = (silu_slope(v.fp[at, :]) * grad).astype(bf16)
+            return carry
+
+        lax.fori_loop(0, S, encode_back, 0)
+        third.stage(2)
+        fourth.stage(1)
+        fifth.full[:, self.c_in :] = jnp.zeros((D, N_IN - self.c_in), f32)
+        for s in range(S):
+            grad = mm_tn(v.dt[s * C : (s + 1) * C, :], x[s])
+            if s:
+                grad = grad + fifth.full[:, : self.c_in]
+            fifth.full[:, : self.c_in] = grad
+        fifth.stage(0)
+        first.stage(4)
+        second.stage(4)
+        loss_sum.finish("x")
+        loss_sum.start("y")
+        third.stage(3)
+        fourth.stage(2)
+        fifth.stage(1)
+        first.stage(5)
+        second.stage(5)
+        third.stage(4)
+        fourth.stage(3)
+        fifth.stage(2)
+        loss_sum.finish("y")
+        loss_sum.start("z")
+        first.stage(6)
+        outs[0][...] = first.out[...]
+        second.stage(6)
+        outs[1][...] = second.out[...]
+        third.stage(5)
+        fourth.stage(4)
+        fifth.stage(3)
+        third.stage(6)
+        outs[2][...] = third.out[...]
+        fourth.stage(5)
+        fifth.stage(4)
+        fourth.stage(6)
+        outs[3][...] = fourth.out[...]
+        fifth.stage(5)
+        loss_sum.finish("z")
+        stats[...] = loss_sum.value[...] / (C_OUT * S * area_sum.value[...])
+        fifth.stage(6)
+        outs[4][...] = fifth.out[...]
+
+        for i in range(8):
+            w_copy(i, 0).wait_send()
+            for d in hops:
+                w_copy(i, 1, d).wait_send()
+                w_copy(i, 2, d).wait_send()
+        for s in range(S):
+            for d in range(1, Z):
+                mz(s, d).wait_send()
+                dz(s, d).wait_send()
+            for d in range(1, Y):
+                for e in range(Z):
+                    my(s, d, e).wait_send()
+                dy(s, d).wait_send()
+            for copy in (mr, ac):
+                copy(s, 0).wait_send()
+                for d in hops:
+                    copy(s, 1, d).wait_send()
+                    copy(s, 2, d).wait_send()
+            for xx in range(X):
+                pk(1, s, xx).wait_send()
+            for d in hops:
+                px(1, s, d).wait_send()
+        area_sum.drain()
+        loss_sum.drain()
+        for chunk in self.chunks:
+            chunk.drain()
+
+    def __call__(self, count, x, tgt, area, node, snd, rcv, wit, wl, wo):
+        vm = pl.BlockSpec(memory_space=pltpu.VMEM)
+        return pl.pallas_call(
+            self.kernel,
+            out_shape=[jax.ShapeDtypeStruct((self.SH, c.w), c.late) for c in self.chunks] + [jax.ShapeDtypeStruct((8, 128), f32)],
+            in_specs=[pl.BlockSpec(memory_space=pltpu.SMEM)] + [vm] * 7 + [pl.BlockSpec(memory_space=pl.ANY), vm],
+            out_specs=[vm] * 6,
+            scratch_shapes=self.scratch(),
+            name="train_step",
+            compiler_params=pltpu.CompilerParams(collective_id=0, has_side_effects=True, vmem_limit_bytes=67043328),
+        )(count, x, tgt, area, node, snd, rcv, wit, wl, wo)
+
+
+def kernel_body(
+    mesh,
     inputs,
     targets,
     cell_area,
@@ -70,12 +924,41 @@
     weight_input,
     weight_latent,
     weight_output,
-    mean_input,
-    mean_latent,
-    mean_output,
-    square_input,
-    square_latent,
-    square_output,
+):
+    samples, slots, c_in = inputs.shape
+    dim = weight_latent.shape[2]
+    step = Step(mesh, samples, slots, dim, edge_senders.shape[0], c_in)
+    wit = jnp.pad(weight_input.T.astype(bf16), ((0, 0), (0, N_IN - c_in)))
+    one, two, three, four, five, stats = step(
+        cell_count,
+        inputs,
+        targets,
+        cell_area[None, :],
+        cell_node[None, :],
+        edge_senders[None, :],
+        edge_receivers[None, :],
+        wit,
+        weight_latent,
+        weight_output,
+    )
+    two, three, four = (g.astype(f32) for g in (two, three, four))
+    gradient_latent = jnp.stack(
+        [four[:, :dim], three[:, :dim], three[:, dim : 2 * dim], two[:, dim : 2 * dim], two[:, :dim], one[:, :dim]]
+    )
+    return stats[0, 0], five[:, :c_in].T, gradient_latent, one[:, dim : dim + C_OUT]
+
+
+def native_gradients(
+    inputs,
+    targets,
+    cell_area,
+    cell_count,
+    cell_node,
+    edge_senders,
+    edge_receivers,
+    weight_input,
+    weight_latent,
+    weight_output,
 ):
     full_input, complete_latent, full_output = (
         lax.all_gather(weight_input.astype(jnp.bfloat16), "col", axis=1, tiled=True),
@@ -195,6 +1078,34 @@
     gradient_input = lax.dynamic_slice_in_dim(whole_input, column * width_input, width_input, 1)
     gradient_latent = lax.dynamic_slice_in_dim(whole_latent, column * width_latent, width_latent, 1)
     gradient_output = lax.dynamic_slice_in_dim(whole_output, column * width_output, width_output, 0)
+    return loss_value, gradient_input, gradient_latent, gradient_output
+
+
+def body(
+    mesh,
+    inputs,
+    targets,
+    cell_area,
+    cell_count,
+    cell_node,
+    edge_senders,
+    edge_receivers,
+    weight_input,
+    weight_latent,
+    weight_output,
+    mean_input,
+    mean_latent,
+    mean_output,
+    square_input,
+    square_latent,
+    square_output,
+):
+    given = (inputs, targets, cell_area, cell_count, cell_node, edge_senders, edge_receivers, weight_input, weight_latent, weight_output)
+    step = Step(mesh, inputs.shape[0], inputs.shape[1], weight_latent.shape[2], edge_senders.shape[0], inputs.shape[2])
+    if step.vmem_bytes() < VMEM_ROOM:
+        loss_value, gradient_input, gradient_latent, gradient_output = kernel_body(mesh, *given)
+    else:
+        loss_value, gradient_input, gradient_latent, gradient_output = native_gradients(*given)
     first_input, second_input, update_input = adam_parts(
         weight_input, gradient_input, mean_input, square_input
     )
@@ -265,7 +1176,7 @@
         P("col", None),
     )
     return jax.shard_map(
-        body,
+        functools.partial(body, mesh),
         mesh=mesh,
         in_specs=placed,
         out_specs=(

time: 700 us -> 205 us (0.29)
  waiting for transfers between devices: 425 us -> 0 us
  matrix products: 152 us -> 0 us
  Pallas kernels: 0 us -> 148 us
  blocking collectives: 59.5 us -> 5.76 us
  between operations: 20.6 us -> 2.89 us
  local copies, waits for them, and re-layouts: 15.9 us -> 28.9 us
    unnamed x11 -> x0, waiting for transfers between devices: 164 us -> none
    psum x1 -> x0, waiting for transfers between devices: 162 us -> none  [body(): lax.psum((local_terms[0], local_terms[1], local_terms[2]), ('row', 'col'))]
    dot_general x43 -> x0, matrix products: 152 us -> none  [the longest x42 151 us: reduced_matmul(): return jnp.einsum(form, left, right, preferred_element_type=jnp.float32)]
    pallas_call x0 -> x1, Pallas kernels: none -> 148 us  [__call__(): pl.pallas_call(self.kernel, out_shape=[jax.ShapeDtypeStruct((self.SH, c.w...]
    all_gather x4 -> x0, waiting for transfers between devices: 98.8 us -> none  [the longest x1 40 us: body(): lax.all_gather(mesh_state_reduced, 'row', axis=1, tiled=True)]
    psum x1 -> x0, blocking collectives: 39.6 us -> none  [body(): lax.psum(jnp.sum(weighted * error), ('row', 'col')) / denominator]
    unnamed x86 -> x50, local copies, waits for them, and re-layouts: 5.7 us -> 22.9 us
    all_gather x2 -> x0, blocking collectives: 13 us -> none  [the longest x1 7.11 us: body(): lax.all_gather(weight_input.astype(jnp.bfloat16), 'col', axis=1, tiled=True)]
  transfers between devices with their start and end apart: 8 -> 0, of which waited for: 8 -> 0; matrix products, arithmetic and copies ran while one was open for 5% -> 0% of each run, Pallas kernels for 0% -> 0%
where the time goes in v1:
time: 205 us; the launch traced here: 204 us
  Pallas kernels  148 us (72%)
  local copies, waits for them, and re-layouts  28.9 us (14%)
  other arithmetic  18.8 us (9%)
  blocking collectives  5.76 us (3%)
  between operations  2.89 us (1%)
    pallas_call x1, Pallas kernels, __call__(): pl.pallas_call(self.kernel, out_shape=[jax.ShapeDtypeStruct((self.SH, c.w...  148 us
    unnamed x50, local copies, waits for them, and re-layouts  22.9 us
    psum x1, blocking collectives, body(): norm_sums = lax.psum(jnp.stack([weight_sums, update_sums]), 'col')  5.76 us
    reduce_sum x1, other arithmetic, body(): jnp.sum(weight_latent * weight_latent, axis=(1, 2))  4.26 us

profile of v1, /device:TPU:0, one launch (start us, length us, event | category | flops | bytes accessed | tf_op | source)
XLA Modules:
  0.0 204.3 jit_solution(13820761936061249282)
XLA Ops:
  0.7 0.0 copy-start.11
  0.7 0.0 copy-start.5
  1.4 1.4 multiply_reduce_fusion.5
  2.8 1.2 broadcast_in_dim.25.area
  4.1 1.2 broadcast_in_dim.26.node
  5.3 1.6 multiply_reduce_fusion.3
  6.9 0.1 copy.55
  7.0 0.6 pad.4.wit
  7.7 1.5 copy.58.wo
  9.2 1.5 copy.60
  10.7 1.5 copy.62
  12.2 1.7 copy.65
  13.9 1.7 copy.59
  15.5 1.7 copy.61
  17.2 0.0 copy-done.11
  17.2 1.0 copy.57.tgt
  18.2 0.0 copy-done.5
  18.2 1.5 copy.56.x
  19.7 147.9 %train_step.1 = (f32[128,640]{1,0:T(8,128)}, bf16[128,1024]{1,0:T(8,128)(2,1)}, bf16[128,1024]{1,0:T(8,128)(2,1)}, bf16[128,512]{1,0:T(8,128)(2,1)}, f32[128,256]{1,0:T(8,128)}, /*index=5*/f32[8,128]{1,0:T(8,128)}) custom-call(s32[1]{0:T(128)S(6)} %copy.82.count, bf16[4,384,227]{2,1,0:T(8,128)(2,1)} %copy.56.x, bf16[4,384,83]{2,1,0:T(8,128)(2,1)} %copy.57.tgt, ...), custom_call_target="tpu_custom_call" | custom-call | tf_op jit(solution)/shard_map/train_step/pallas_call | solution.py:904
  167.6 0.0 copy-start.10
  167.6 1.2 slice.42
  168.8 0.0 copy-start.9
  168.8 1.8 multiply_reduce_fusion.2
  170.7 0.9 slice_bitcast_fusion.4
  171.6 0.0 copy-start.12
  171.6 0.7 copy.67
  172.3 1.6 multiply_reduce_fusion.4
  173.9 0.0 copy-start.6
  173.9 0.0 copy-start.7
  173.9 0.7 copy.68
  174.6 0.7 copy.72
  175.4 0.7 copy.70
  176.1 0.7 copy.71
  176.8 0.7 copy.69
  177.6 0.0 copy-done.10
  177.6 0.0 copy-done.6
  177.6 0.0 copy-done.7
  177.6 0.0 copy-done.9
  177.6 0.0 copy-start.8
  177.6 0.0 copy-start.3
  177.7 0.0 copy-done.12
  177.7 0.0 copy-start
  177.9 0.7 copy-done.8
  178.6 0.5 copy-done.3
  179.2 0.5 copy-done
  179.6 0.0 copy-start.2
  179.6 0.0 copy-start.4
  179.6 4.3 %multiply_reduce_fusion.1 = (f32[6]{0:T(128)S(1)}, f32[6]{0:T(128)S(1)}, f32[6,128,512]{2,1,0:T(8,128)S(1)}, f32[6,128,512]{2,1,0:T(8,128)}) fusion(f32[6,128,512]{2,1,0:T(8,128)S(1)} %copy-done, f32[6,128,512]{2,1,0:T(8,128)S(1)} %bitcast_dynamic-update-slice_fusion, f32[6,128,512]{2,1,0:T(8,128)S(1)} %copy-done.3, f32[6,128,512]{2,1,0:T(8,128)} %param.27), kind=kLoop, calls=%fused_computation.6 | loop fusion | flops 5505012 | bytes 9437232 | tf_op jit(solution)/shard_map/reduce_sum | solution.py:1121
  183.9 0.0 copy-done.2
  183.9 0.0 copy-start.1
  183.9 2.7 %maximum_bitcast_fusion = (f32[1,8]{1,0:T(1,128)S(1)}, f32[1,8]{1,0:T(1,128)S(1)}) fusion(f32[1]{0:T(128)} %bitcast.12, f32[6]{0:T(128)S(1)} %get-tuple-element.63, f32[1]{0:T(128)} %bitcast.11, f32[1]{0:T(128)} %bitcast.15, f32[6]{0:T(128)S(1)} %get-tuple-element.64, f32[1]{0:T(128)} %bitcast.14), kind=kLoop, calls=%fused_computation.33 | loop fusion | flops 32 | bytes 128 | tf_op jit(solution)/shard_map/stack | solution.py:1132
  186.6 5.8 %psum.7 = f32[2,8]{1,0:T(2,128)S(1)} all-reduce(f32[2,8]{1,0:T(2,128)S(1)} %pad_maximum_fusion), channel_id=1, replica_groups=mesh['row'=8,'col'=4] {'col'}, use_global_device_ids=true, to_apply=%region_6.7 | all-reduce | flops 16 | bytes 128 | tf_op jit(solution)/shard_map/psum | solution.py:1132
  192.4 0.1 multiply_bitcast_fusion
  192.4 0.6 fusion.13
  194.3 0.0 copy-done.4
  194.3 0.7 fusion.9
  195.1 1.0 fusion.7
  196.0 0.7 copy.76
  196.8 1.6 copy.75
  198.3 0.7 copy.74
  199.0 1.6 copy.73
  200.7 3.6 %fusion.8 = (bf16[6,128,512]{2,1,0:T(8,128)(2,1)}, f32[6,128,512]{2,1,0:T(8,128)}) fusion(f32[6,128,512]{2,1,0:T(8,128)S(1)} %copy-done, f32[6,128,512]{2,1,0:T(8,128)} %get-tuple-element.75, f32[6,128,512]{2,1,0:T(8,128)S(1)} %get-tuple-element.74, f32[6]{0:T(128)S(1)} %multiply_bitcast_fusion), kind=kLoop, calls=%fused_computation.38 | loop fusion | flops 2752512 | bytes 7077912 | tf_op jit(solution)/shard_map/convert_element_type | solution.py:1153
  204.3 0.0 copy-done.1
  204.3 0.0 copy-done.13
  (12 shorter events, 0.2 us)
Async XLA Ops:
  0.7 16.5 %copy-start.11 = (bf16[4,384,83]{1,0,2:T(4,128)(2,1)S(1)}, bf16[4,384,83]{1,0,2:T(4,128)(2,1)}, u32[]{:S(2)}) copy-start(bf16[4,384,83]{1,0,2:T(4,128)(2,1)} %param.17) | copy-start | bytes 764932
  0.7 17.5 %copy-start.5 = (bf16[4,384,227]{1,0,2:T(4,128)(2,1)S(1)}, bf16[4,384,227]{1,0,2:T(4,128)(2,1)}, u32[]{:S(2)}) copy-start(bf16[4,384,227]{1,0,2:T(4,128)(2,1)} %param.16) | copy-start | bytes 2092036
  167.6 10.0 %copy-start.10 = (bf16[128,1024]{1,0:T(8,128)(2,1)S(1)}, bf16[128,1024]{1,0:T(8,128)(2,1)}, u32[]{:S(2)}) copy-start(bf16[128,1024]{1,0:T(8,128)(2,1)} %get-tuple-element.26) | copy-start | bytes 786436
  168.8 8.8 %copy-start.9 = (bf16[128,1024]{1,0:T(8,128)(2,1)S(1)}, bf16[128,1024]{1,0:T(8,128)(2,1)}, u32[]{:S(2)}) copy-start(bf16[128,1024]{1,0:T(8,128)(2,1)} %get-tuple-element.27) | copy-start | bytes 786436
  171.6 6.1 %copy-start.12 = (bf16[128,512]{1,0:T(8,128)(2,1)S(1)}, bf16[128,512]{1,0:T(8,128)(2,1)}, u32[]{:S(2)}) copy-start(bf16[128,512]{1,0:T(8,128)(2,1)} %get-tuple-element.25) | copy-start | bytes 393220
  173.9 3.7 %copy-start.6 = (f32[128,83]{1,0:T(8,128)}, f32[128,83]{1,0:T(8,128)S(1)}, u32[]{:S(2)}) copy-start(f32[128,83]{1,0:T(8,128)S(1)} %get-tuple-element.77) | copy-start | bytes 127492
  173.9 3.7 %copy-start.7 = (f32[128,83]{1,0:T(8,128)}, f32[128,83]{1,0:T(8,128)S(1)}, u32[]{:S(2)}) copy-start(f32[128,83]{1,0:T(8,128)S(1)} %get-tuple-element.78) | copy-start | bytes 127492
  177.6 1.0 copy-start.8
  177.6 1.5 copy-start.3
  177.7 1.9 copy-start
  179.6 4.3 %copy-start.2 = (f32[6,128,512]{2,1,0:T(8,128)}, f32[6,128,512]{2,1,0:T(8,128)S(1)}, u32[]{:S(2)}) copy-start(f32[6,128,512]{2,1,0:T(8,128)S(1)} %bitcast_dynamic-update-slice_fusion) | copy-start | bytes 4718596
  179.6 14.7 %copy-start.4 = (f32[227,128]{0,1:T(8,128)S(1)}, f32[227,128]{0,1:T(8,128)}, u32[]{:S(2)}) copy-start(f32[227,128]{0,1:T(8,128)} %copy.65) | copy-start | bytes 348676
  183.9 20.4 %copy-start.1 = (f32[6,128,512]{2,1,0:T(8,128)}, f32[6,128,512]{2,1,0:T(8,128)S(1)}, u32[]{:S(2)}) copy-start(f32[6,128,512]{2,1,0:T(8,128)S(1)} %get-tuple-element.74) | copy-start | bytes 4718596
  192.4 11.9 %copy-start.13 = (f32[2,8]{1,0:T(2,128)}, f32[2,8]{1,0:T(2,128)S(1)}, u32[]{:S(2)}) copy-start(f32[2,8]{1,0:T(2,128)S(1)} %sqrt.15) | copy-start | bytes 196

commit v2 on v1

--- a/solution.py
+++ b/solution.py
@@ -196,8 +196,8 @@
             value = value + buf[i]
         self.value[...] = value
 
-    def drain(self):
-        for axis in self.AXES:
+    def drain(self, axes):
+        for axis in axes:
             for copy in self._copies(axis):
                 copy.wait_send()
 
@@ -382,13 +382,11 @@
             dt=vm((S * C, D), bf16),
             av=vm((S * N, D), bf16),
             sp=vm((S * N, D), f32),
-            ml=vm((S * N, D), f32),
             mlb=vm((S * N, D), bf16),
             agb=vm((S * N, D), bf16),
             mnb=vm((S * N, D), bf16),
             sg=vm((S * N, D), f32),
             dmn=vm((S * N, D), f32),
-            dbb=vm((S * N, D), bf16),
             dsb=vm((S * N, D), bf16),
             drb=vm((S * N, D), bf16),
             d2b=vm((S * N, D), bf16),
@@ -409,7 +407,7 @@
             dzs=vm((S, Z - 1, N, D), bf16),
             dzr=vm((S, Z - 1, N, D), bf16),
             loss=vm((8, 128), f32),
-            l_sem=dma(6),
+            l_sem=dma(24),
             w_ss=dma(8, 1 + 2 * (X - 1)),
             w_rs=dma(8, 1 + 2 * (X - 1)),
             mz_ss=dma(S, Z - 1),
@@ -443,17 +441,17 @@
 
     def scratch(self):
         total = Total.scratch(*self.grid)
-        return [*self.shapes.values(), *total, *total, *[s for c in self.chunks for s in c.scratch()]]
-
-    def kernel(self, count, x, tgt, area, node, snd, rcv, wit, wl, wo, *refs):
+        return [*self.shapes.values(), *total * 3, *[s for c in self.chunks for s in c.scratch()]]
+
+    def kernel(self, count, x, tgt, area, node, snd, rcv, wi, wl, wo, mi, mal, mo, si, sal, so, *refs):
         S, C, D, E, N, R, Q, SH = self.S, self.C, self.D, self.E, self.N, self.R, self.Q, self.SH
         X, Y, Z = self.grid
-        outs, stats, refs = refs[:5], refs[5], refs[6:]
+        (g_in, g_out, g_skip, g_two, g_three, g_four, stats), refs = refs[:7], refs[7:]
         v = types.SimpleNamespace(**dict(zip(self.shapes, refs)))
         refs = refs[len(self.shapes) :]
         p = Place(self.n_row, self.n_col)
-        area_sum, loss_sum = Total(p, refs[:7]), Total(p, refs[7:14])
-        refs = refs[14:]
+        area_sum, loss_sum, norm_sum = (Total(p, refs[i : i + 7]) for i in (0, 7, 14))
+        refs = refs[21:]
         for chunk in self.chunks:
             many = len(chunk.scratch())
             chunk.bind(p, refs[:many])
@@ -484,15 +482,20 @@
 
         W = lambda which: v.wlb[which]
         own = ds(p.col * SH, SH)
-        v.wib[own, :] = wit[...]
+
+        def turned(ref, n):
+            v.tmp[0:n, 0:SH] = jnp.zeros((n, SH), f32)
+            v.tmp[0 : ref.shape[0], 0:SH] = ref[...]
+            return jnp.transpose(v.tmp[0:n, 0:SH])
+
+        v.wib[own, :] = turned(wi, N_IN).astype(bf16)
         loads = [pltpu.make_async_copy(wl.at[m], v.fp.at[m * SH : (m + 1) * SH, :], v.l_sem.at[m]) for m in range(6)]
         for load in loads:
             load.start()
         for m, load in enumerate(loads):
             load.wait()
             v.wlb[m, own, :] = v.fp[m * SH : (m + 1) * SH, :].astype(bf16)
-        v.wob[own, :] = jnp.zeros((SH, N_OUT), bf16)
-        v.wob[own, 0:C_OUT] = wo[...].astype(bf16)
+        v.wob[own, :] = turned(wo, N_OUT).astype(bf16)
         p.barrier()
         for i in range(8):
             w_copy(i, 0).start()
@@ -500,14 +503,14 @@
                 w_copy(i, 1, d).start()
 
         used = count[0]
-        node_row = node[...]
+        node_row = node[...].reshape(1, C)
         match = (lax.broadcasted_iota(jnp.int32, (N, C), 0) == node_row).astype(f32)
         v.nm[...] = match.astype(bf16)
         match = match * (lax.broadcasted_iota(jnp.int32, (N, C), 1) < used).astype(f32)
         v.nv[...] = match.astype(bf16)
         v.cnt[...] = jnp.broadcast_to(jnp.maximum(jnp.sum(match, axis=1, keepdims=True), 1.0), (N, 128))
         node_col = jnp.transpose(jnp.broadcast_to(node_row, (128, C)))
-        area_row = area[...] * (lax.broadcasted_iota(jnp.int32, (1, C), 1) < used).astype(f32)
+        area_row = area[...].reshape(1, C) * (lax.broadcasted_iota(jnp.int32, (1, C), 1) < used).astype(f32)
         v.cw[...] = jnp.transpose(jnp.broadcast_to(area_row, (128, C)))
         match = (lax.broadcasted_iota(jnp.int32, (C, 128), 1) == node_col).astype(f32)
         v.cm[...] = match[:, :N].astype(bf16)
@@ -535,8 +538,7 @@
         w_get(1)
         pre = mm(v.av[...], W(0))
         v.sp[...] = pre
-        v.ml[...] = silu(pre)
-        v.mlb[...] = v.ml[...].astype(bf16)
+        v.mlb[...] = silu(pre).astype(bf16)
         w_forward(2)
         w_get(2)
         v.tmp[0 : S * N, :] = mm(v.mlb[...], W(1))
@@ -672,7 +674,7 @@
         for s in range(S):
             v.agb[s * N : (s + 1) * N, :] = (col_last(0, s) * (1.0 / DEG)).astype(bf16)
 
-        v.mnb[...] = (v.ml[...] + mm(v.agb[...], W(3))).astype(bf16)
+        v.mnb[...] = (silu(v.sp[...]) + mm(v.agb[...], W(3))).astype(bf16)
         w_get(6)
         w_get(7)
         v.dp[...] = jnp.zeros((S * C, N_OUT), bf16)
@@ -696,8 +698,7 @@
         lax.fori_loop(0, S, decode, 0)
         high, low = high_low(v.sg[...])
         v.dmn[...] = mm_nt(high, W(4)) + mm_nt(low, W(4))
-        v.dbb[...] = v.dmn[...].astype(bf16)
-        v.tmp[0 : S * N, :] = mm_nt(v.dbb[...], W(3))
+        v.tmp[0 : S * N, :] = mm_nt(v.dmn[...].astype(bf16), W(3))
         for s in range(S):
             v.da[s, ds(p.col * N, N), :] = v.tmp[s * N : (s + 1) * N, :].astype(bf16)
 
@@ -720,7 +721,7 @@
         first.stage(0)
         high, low = high_low(v.sg[...])
         second.full[:, 0:D] = mm_tn(v.mnb[...], high) + mm_tn(v.mnb[...], low)
-        second.full[:, D : 2 * D] = mm_tn(v.agb[...], v.dbb[...])
+        second.full[:, D : 2 * D] = mm_tn(v.agb[...], v.dmn[...].astype(bf16))
         second.stage(0)
 
         def skip_back(at):
@@ -799,6 +800,13 @@
             return carry
 
         lax.fori_loop(0, S + 1, backward, 0)
+        states = [
+            pltpu.make_async_copy(a.at[m], v.ep.at[j, m * SH : (m + 1) * SH, :], v.l_sem.at[6 + 6 * j + m])
+            for j, a in enumerate((wl, mal, sal))
+            for m in range(6)
+        ]
+        for load in states:
+            load.start()
         first.stage(2)
         second.stage(2)
         for s in range(S):
@@ -853,24 +861,52 @@
         fifth.stage(2)
         loss_sum.finish("y")
         loss_sum.start("z")
+        for load in states:
+            load.wait()
+        lane = lax.broadcasted_iota(jnp.int32, (8, 128), 1)
+        row = lax.broadcasted_iota(jnp.int32, (8, 128), 0)
+        norm_sum.value[...] = jnp.zeros((8, 128), f32)
+
+        def note(j, weight, gradient, mean, square):
+            _, _, update = adam_parts(weight, gradient, mean, square)
+            for i, what in enumerate((weight, update)):
+                norm_sum.value[...] += jnp.where((row == i) & (lane == j), jnp.sum(what * what), 0.0)
+
+        def note_latent(m, gradient):
+            weight, mean, square = (v.ep[j, m * SH : (m + 1) * SH, :] for j in range(3))
+            note(1 + m, weight, gradient.astype(f32), mean, square)
+
         first.stage(6)
-        outs[0][...] = first.out[...]
+        g_skip[...] = first.out[:, :D]
+        g_out[...] = jnp.transpose(first.out[:, D : D + N_OUT])[: g_out.shape[0], :]
         second.stage(6)
-        outs[1][...] = second.out[...]
+        g_two[...] = second.out[:, : 2 * D]
         third.stage(5)
         fourth.stage(4)
         fifth.stage(3)
+        note_latent(5, first.out[:, :D])
+        note(7, wo[...], g_out[...], mo[...], so[...])
+        note_latent(4, second.out[:, 0:D])
+        note_latent(3, second.out[:, D : 2 * D])
         third.stage(6)
-        outs[2][...] = third.out[...]
+        g_three[...] = third.out[:, : 2 * D]
         fourth.stage(5)
         fifth.stage(4)
+        note_latent(1, third.out[:, 0:D])
+        note_latent(2, third.out[:, D : 2 * D])
         fourth.stage(6)
-        outs[3][...] = fourth.out[...]
+        g_four[...] = fourth.out[:, :D]
         fifth.stage(5)
+        note_latent(0, fourth.out[:, :D])
         loss_sum.finish("z")
-        stats[...] = loss_sum.value[...] / (C_OUT * S * area_sum.value[...])
         fifth.stage(6)
-        outs[4][...] = fifth.out[...]
+        g_in[...] = jnp.transpose(fifth.out[:, :N_IN])[: g_in.shape[0], :]
+        note(0, wi[...], g_in[...], mi[...], si[...])
+        norm_sum.start("k")
+        norm_sum.finish("k")
+        norm_sum.start("x")
+        norm_sum.finish("x")
+        stats[...] = jnp.where(row < 2, norm_sum.value[...], loss_sum.value[...] / (C_OUT * S * area_sum.value[...]))
 
         for i in range(8):
             w_copy(i, 0).wait_send()
@@ -894,58 +930,96 @@
                 pk(1, s, xx).wait_send()
             for d in hops:
                 px(1, s, d).wait_send()
-        area_sum.drain()
-        loss_sum.drain()
+        area_sum.drain("kxyz")
+        loss_sum.drain("kxyz")
+        norm_sum.drain("kx")
         for chunk in self.chunks:
             chunk.drain()
 
-    def __call__(self, count, x, tgt, area, node, snd, rcv, wit, wl, wo):
-        vm = pl.BlockSpec(memory_space=pltpu.VMEM)
+    def __call__(self, count, x, tgt, area, node, snd, rcv, *states):
+        vm, hbm = pl.BlockSpec(memory_space=pltpu.VMEM), pl.BlockSpec(memory_space=pl.ANY)
+        D, SH = self.D, self.SH
+        outs = [(states[0].shape, f32), (states[2].shape, f32), ((SH, D), f32), ((SH, 2 * D), bf16), ((SH, 2 * D), bf16), ((SH, D), bf16), ((8, 128), f32)]
         return pl.pallas_call(
             self.kernel,
-            out_shape=[jax.ShapeDtypeStruct((self.SH, c.w), c.late) for c in self.chunks] + [jax.ShapeDtypeStruct((8, 128), f32)],
-            in_specs=[pl.BlockSpec(memory_space=pltpu.SMEM)] + [vm] * 7 + [pl.BlockSpec(memory_space=pl.ANY), vm],
-            out_specs=[vm] * 6,
+            out_shape=[jax.ShapeDtypeStruct(*o) for o in outs],
+            in_specs=[pl.BlockSpec(memory_space=pltpu.SMEM)] + [vm] * 6 + [vm, hbm, vm] * 3,
+            out_specs=[vm] * 7,
             scratch_shapes=self.scratch(),
             name="train_step",
             compiler_params=pltpu.CompilerParams(collective_id=0, has_side_effects=True, vmem_limit_bytes=67043328),
-        )(count, x, tgt, area, node, snd, rcv, wit, wl, wo)
-
-
-def kernel_body(
-    mesh,
-    inputs,
-    targets,
-    cell_area,
-    cell_count,
-    cell_node,
-    edge_senders,
-    edge_receivers,
-    weight_input,
-    weight_latent,
-    weight_output,
-):
-    samples, slots, c_in = inputs.shape
-    dim = weight_latent.shape[2]
-    step = Step(mesh, samples, slots, dim, edge_senders.shape[0], c_in)
-    wit = jnp.pad(weight_input.T.astype(bf16), ((0, 0), (0, N_IN - c_in)))
-    one, two, three, four, five, stats = step(
-        cell_count,
-        inputs,
-        targets,
-        cell_area[None, :],
-        cell_node[None, :],
-        edge_senders[None, :],
-        edge_receivers[None, :],
-        wit,
-        weight_latent,
-        weight_output,
-    )
-    two, three, four = (g.astype(f32) for g in (two, three, four))
-    gradient_latent = jnp.stack(
-        [four[:, :dim], three[:, :dim], three[:, dim : 2 * dim], two[:, dim : 2 * dim], two[:, :dim], one[:, :dim]]
-    )
-    return stats[0, 0], five[:, :c_in].T, gradient_latent, one[:, dim : dim + C_OUT]
+        )(count, x, tgt, area, node, snd, rcv, *states)
+
+
+def update_kernel(g_in, g_out, g_skip, g_two, g_three, g_four, stats, wi, wl, wo, mi, mal, mo, si, sal, so, *refs):
+    loss, *outs, norms = refs[:17]
+    in_buf, out_buf, low_buf, in_sem, out_sem = refs[17:]
+    SH, D = g_skip.shape
+    loads = [[pltpu.make_async_copy(a.at[m], in_buf.at[j, m], in_sem.at[j, m]) for j, a in enumerate((wl, mal, sal))] for m in range(6)]
+    order = (5, 4, 3, 2, 1, 0)
+    for m in order:
+        for load in loads[m]:
+            load.start()
+    root = jnp.sqrt(stats[...])
+    norms[...] = root[0:2, 0:8]
+    loss[...] = stats[2:3, 0:1]
+
+    def step(j, weight, gradient, mean, square):
+        first, second, update = adam_parts(weight, gradient, mean, square)
+        ratio = root[0:1, j : j + 1] / (root[1:2, j : j + 1] + trust_epsilon)
+        master = weight - learn_rate * ratio * update
+        return gradient, first, second, master, master.astype(bf16)
+
+    grads = {5: (g_skip, 0), 4: (g_two, 0), 3: (g_two, D), 2: (g_three, D), 1: (g_three, 0), 0: (g_four, 0)}
+    stores = []
+    for m in order:
+        for load in loads[m]:
+            load.wait()
+        ref, at = grads[m]
+        results = step(1 + m, in_buf[0, m], ref[:, at : at + D].astype(f32), in_buf[1, m], in_buf[2, m])
+        for j, result in enumerate(results):
+            buf = low_buf.at[m] if j == 4 else out_buf.at[j, m]
+            buf[...] = result
+            stores.append(pltpu.make_async_copy(buf, outs[3 * j + 1].at[m], out_sem.at[j, m]))
+            stores[-1].start()
+    for j, result in enumerate(step(0, wi[...], g_in[...], mi[...], si[...])):
+        outs[3 * j][...] = result
+    for j, result in enumerate(step(7, wo[...], g_out[...], mo[...], so[...])):
+        outs[3 * j + 2][...] = result
+    for store in stores:
+        store.wait()
+
+
+def update_all(grads, states):
+    vm, hbm = pl.BlockSpec(memory_space=pltpu.VMEM), pl.BlockSpec(memory_space=pl.ANY)
+    kinds = [f32] * 4 + [bf16]
+    shapes = [states[0].shape, states[1].shape, states[2].shape]
+    n, SH, D = states[1].shape
+    return pl.pallas_call(
+        update_kernel,
+        out_shape=[jax.ShapeDtypeStruct((1, 1), f32)]
+        + [jax.ShapeDtypeStruct(s, k) for k in kinds for s in shapes]
+        + [jax.ShapeDtypeStruct((2, 8), f32)],
+        in_specs=[vm] * 7 + [vm, hbm, vm] * 3,
+        out_specs=[vm] + [vm, hbm, vm] * 5 + [vm],
+        scratch_shapes=[
+            pltpu.VMEM((3, n, SH, D), f32),
+            pltpu.VMEM((4, n, SH, D), f32),
+            pltpu.VMEM((n, SH, D), bf16),
+            pltpu.SemaphoreType.DMA((3, n)),
+            pltpu.SemaphoreType.DMA((5, n)),
+        ],
+        name="lamb",
+        compiler_params=pltpu.CompilerParams(vmem_limit_bytes=67043328),
+    )(*grads, *states)
+
+
+def kernel_body(mesh, step, inputs, targets, cell_area, cell_count, cell_node, edge_senders, edge_receivers, *states):
+    states = [a.T if i % 3 == 2 else a for i, a in enumerate(states)]
+    grads = step(cell_count, inputs, targets, cell_area, cell_node, edge_senders[None, :], edge_receivers[None, :], *states)
+    loss, *outs, norms = update_all(grads, states)
+    outs = [a.T if i % 3 == 2 else a for i, a in enumerate(outs)]
+    return (loss[0, 0], *outs, norms)
 
 
 def native_gradients(
@@ -1101,11 +1175,11 @@
     square_output,
 ):
     given = (inputs, targets, cell_area, cell_count, cell_node, edge_senders, edge_receivers, weight_input, weight_latent, weight_output)
+    states = (mean_input, mean_latent, mean_output, square_input, square_latent, square_output)
     step = Step(mesh, inputs.shape[0], inputs.shape[1], weight_latent.shape[2], edge_senders.shape[0], inputs.shape[2])
     if step.vmem_bytes() < VMEM_ROOM:
-        loss_value, gradient_input, gradient_latent, gradient_output = kernel_body(mesh, *given)
-    else:
-        loss_value, gradient_input, gradient_latent, gradient_output = native_gradients(*given)
+        return kernel_body(mesh, step, *given, *states)
+    loss_value, gradient_input, gradient_latent, gradient_output = native_gradients(*given)
     first_input, second_input, update_input = adam_parts(
         weight_input, gradient_input, mean_input, square_input
     )

time: 205 us -> 163 us (0.80)
  local copies, waits for them, and re-layouts: 28.9 us -> 4.1 us
  other arithmetic: 18.8 us -> 0 us
  Pallas kernels: 148 us -> 157 us
  blocking collectives: 5.76 us -> 0 us
    unnamed x50 -> x2, local copies, waits for them, and re-layouts: 22.9 us -> 4.1 us
    reduce_sum x5 -> x0, other arithmetic: 10.7 us -> none  [the longest x1 4.26 us: body(): jnp.sum(weight_latent * weight_latent, axis=(1, 2))]
    pallas_call x1 -> x2, Pallas kernels: 148 us -> 157 us  [the longest x1 151 us: __call__(): pl.pallas_call(self.kernel, out_shape=[jax.ShapeDtypeStruct(*o) for o in...]
    psum x1 -> x0, blocking collectives: 5.76 us -> none  [body(): norm_sums = lax.psum(jnp.stack([weight_sums, update_sums]), 'col')]
    convert_element_type x5 -> x0, other arithmetic: 5.35 us -> none  [the longest x1 3.57 us: body(): master_latent.astype(jnp.bfloat16)]
    another operation x2 -> x0, other arithmetic: 2.67 us -> none  [body(): norm_sums = lax.psum(jnp.stack([weight_sums, update_sums]), 'col')]
    broadcast_in_dim x2 -> x0, local copies, waits for them, and re-layouts: 2.49 us -> none  [the longest x1 1.24 us: kernel_body(): cell_node[None, :]]
where the time goes in v2:
time: 163 us
  Pallas kernels  157 us (96%)
  local copies, waits for them, and re-layouts  4.1 us (3%)
    pallas_call x1, Pallas kernels, __call__(): pl.pallas_call(self.kernel, out_shape=[jax.ShapeDtypeStruct(*o) for o in...  151 us
    pallas_call x1, Pallas kernels, update_all(): pl.pallas_call(update_kernel, out_shape=[jax.ShapeDtypeStruct((1, 1), f32...  6.82 us
    unnamed x2, local copies, waits for them, and re-layouts  4.1 us

profile of v2, /device:TPU:0, one launch (start us, length us, event | category | flops | bytes accessed | tf_op | source)
XLA Modules:
  0.0 163.0 jit_solution(557923749373465584)
XLA Ops:
  1.3 1.9 %copy.34.tgt = bf16[4,384,83]{2,1,0:T(8,128)(2,1)} copy(bf16[4,384,83]{1,0,2:T(4,128)(2,1)} %param.17) | data formatting | bytes 509952 | tf_op args[1]
  3.2 2.2 %copy.33.x = bf16[4,384,227]{2,1,0:T(8,128)(2,1)} copy(bf16[4,384,227]{1,0,2:T(4,128)(2,1)} %param.16) | data formatting | bytes 1394688 | tf_op args[0]
  5.4 150.6 %train_step.1 = (f32[227,128]{1,0:T(8,128)}, f32[83,128]{1,0:T(8,128)}, f32[128,512]{1,0:T(8,128)}, bf16[128,1024]{1,0:T(8,128)(2,1)}, bf16[128,1024]{1,0:T(8,12...) custom-call(s32[1]{0:T(128)S(6)} %copy.35.count, bf16[4,384,227]{2,1,0:T(8,128)(2,1)} %copy.33.x, ...), custom_call_target="tpu_custom_call" | custom-call | tf_op jit(solution)/shard_map/train_step/pallas_call | solution.py:943
  156.0 6.8 %lamb.1 = (f32[1,1]{1,0:T(1,128)}, f32[227,128]{1,0:T(8,128)}, f32[6,128,512]{2,1,0:T(8,128)}, f32[83,128]{1,0:T(8,128)}, f32[227,128]{1,0:T(8,128)}, /*index=5*...) custom-call(f32[227,128]{1,0:T(8,128)} %get-tuple-element.41.g_in, ...), custom_call_target="tpu_custom_call" | custom-call | tf_op jit(solution)/shard_map/lamb/pallas_call | solution.py:998

commit v3 on v2

--- a/solution.py
+++ b/solution.py
@@ -96,12 +96,12 @@
         at[axis] = self.to(axis, d)
         return (at["z"] * self.Y + at["y"], at["x"] * 2 + at["k"])
 
-    def barrier(self):
+    def greet(self):
         sem = pltpu.get_barrier_semaphore()
         peers = [self.peer(a, d) for a in "kxyz" for d in range(1, getattr(self, a.upper()))]
         for peer in peers:
             pl.semaphore_signal(sem, inc=1, device_id=peer, device_id_type=MESH)
-        pl.semaphore_wait(sem, len(peers))
+        return sem, len(peers)
 
 
 def remote(src, dst, send_sem, recv_sem, device):
@@ -203,142 +203,155 @@
 
 
 class Reduce:
-    def __init__(self, grid, dim, n_col, width, late):
+    def __init__(self, grid, dim, n_col, width, late, order, lender=None, lanes=0):
         self.X, self.Y, self.Z = grid
-        self.dim, self.shard, self.late = dim, dim // n_col, late
+        self.dim, self.shard, self.late, self.order = dim, dim // n_col, late, order
         self.ry = self.shard // self.Y
-        self.zr = min(self.ry // 16, self.Z)
-        self.zl = self.Z // self.zr
-        self.rz = self.ry // self.zr
-        self.w = -(-width // (128 * self.zl)) * 128 * self.zl
-        self.wz = self.w // self.zl
+        self.rz = self.ry // self.Z
+        self.w = width
+        self.lender, self.lanes, self.lent = lender, lanes, False
 
     def scratch(self):
         X, Y, Z, w = self.X, self.Y, self.Z, self.w
         many = X + (X - 1) + 2 * (Y - 1) + 2 * (Z - 1)
+        along_x = (X - 1, 1, self.shard, w) if self.order == "xy" else (X - 1, 1, self.ry, w)
+        along_y = (Y - 1, 1, self.ry, w) if self.order == "xy" else (Y - 1, X, self.ry, w)
         return [
-            pltpu.VMEM((self.dim, w), f32),
+            *([] if self.lender else [pltpu.VMEM((self.dim, w), f32)]),
             pltpu.VMEM((X, self.shard, w), f32),
-            pltpu.VMEM((X - 1, self.shard, w), bf16),
-            pltpu.VMEM((X - 1, self.shard, w), bf16),
-            pltpu.VMEM((Y - 1, self.ry, w), bf16),
-            pltpu.VMEM((Y - 1, self.ry, w), bf16),
-            pltpu.VMEM((Z - 1, self.rz, self.wz), self.late),
-            pltpu.VMEM((Z - 1, self.rz, self.wz), self.late),
-            pltpu.VMEM((self.rz, self.wz), f32),
+            pltpu.VMEM(along_x, bf16),
+            pltpu.VMEM(along_x, bf16),
+            pltpu.VMEM(along_y, bf16),
+            pltpu.VMEM(along_y, bf16),
+            pltpu.VMEM((Z - 1, self.rz, w), self.late),
+            pltpu.VMEM((Z - 1, self.rz, w), self.late),
+            pltpu.VMEM((self.rz, w), f32),
             pltpu.VMEM((self.shard, w), self.late),
             pltpu.SemaphoreType.DMA((many,)),
             pltpu.SemaphoreType.DMA((many,)),
         ]
 
     def bind(self, place, refs):
+        if self.lender:
+            refs = (self.lender.full.at[:, self.lanes : self.lanes + self.w], *refs)
         (self.full, self.cr, self.xs, self.xr, self.ys, self.yr, self.zs, self.zin, self.piece, self.out, self.ss, self.rs) = refs
         self.p = place
-        self.copies = []
+
+    def lend(self):
+        for copy in self.copies(0):
+            copy.wait_send()
 
     def rows_of(self, x, k):
         return (2 * x + k) * self.shard
 
-    def piece_at(self, z):
-        rows = pl.multiple_of((z // self.zl) * self.rz, 16)
-        if self.zl == 1:
-            return rows, pl.ds(0, self.wz)
-        return rows, pl.ds(pl.multiple_of((z % self.zl) * self.wz, 128), self.wz)
-
-    def _send(self, i, src, dst, device):
-        copy = remote(src, dst, self.ss.at[i], self.rs.at[i], device)
-        copy.start()
-        self.copies.append(copy)
-        return copy
+    def place_z(self):
+        return pl.ds(pl.multiple_of(self.p.y * self.ry + self.p.z * self.rz, 16), self.rz)
+
+    def copies(self, stage):
+        p, X, Y, Z = self.p, self.X, self.Y, self.Z
+        first_x = self.order == "xy"
+        x_base, y_base = (X, 2 * X - 1) if first_x else (X + Y - 1, X)
+        base = (0, x_base if first_x else y_base, y_base if first_x else x_base, 2 * X + Y - 2, 2 * X + Y + Z - 3, 2 * X + Y + 2 * Z - 4)[stage]
+        if stage == 0:
+            many = [(self.full.at[ds(self.rows_of(x, 1 - p.k), self.shard), :], self.cr.at[x], p.peer("k", 1)) for x in range(X)]
+        elif stage == (1 if first_x else 2):
+            many = [(self.xs.at[d - 1], self.xr.at[d - 1], p.peer("x", d)) for d in range(1, X)]
+        elif stage == (2 if first_x else 1):
+            many = [(self.ys.at[d - 1], self.yr.at[d - 1], p.peer("y", d)) for d in range(1, Y)]
+        elif stage == 3:
+            many = [(self.zs.at[d - 1], self.zin.at[d - 1], p.peer("z", d)) for d in range(1, Z)]
+        elif stage == 4:
+            here = self.out.at[self.place_z(), :]
+            many = [(here, here, p.peer("z", d)) for d in range(1, Z)]
+        else:
+            here = self.out.at[pl.ds(pl.multiple_of(p.y * self.ry, 16), self.ry), :]
+            many = [(here, here, p.peer("y", d)) for d in range(1, Y)]
+        return [remote(src, dst, self.ss.at[base + i], self.rs.at[base + i], to) for i, (src, dst, to) in enumerate(many)]
+
+    def sum_core(self, x, at, n=16):
+        mine = self.full[pl.ds(pl.multiple_of(self.rows_of(x, self.p.k) + at, 16), n), :]
+        return mine + self.cr[x, pl.ds(at, n), :]
+
+    def sum_first(self, x, y, at):
+        rows = pl.multiple_of(y * self.ry + at, 16)
+        value = self.sum_core(x, rows)
+        if self.order == "xy":
+            for d in range(1, self.X):
+                value = value + self.xr[d - 1, 0, pl.ds(rows, 16), :].astype(f32)
+        else:
+            for d in range(1, self.Y):
+                value = value + self.yr[d - 1, x, pl.ds(at, 16), :].astype(f32)
+        return value
 
     def stage(self, s):
         p, X, Y, Z = self.p, self.X, self.Y, self.Z
-        if s == 0:
-            self.core = [
-                self._send(x, self.full.at[ds(self.rows_of(x, 1 - p.k), self.shard), :], self.cr.at[x], p.peer("k", 1))
-                for x in range(X)
-            ]
-        elif s == 1:
-            for copy in self.core:
+        if s:
+            for copy in self.copies(s - 1):
                 copy.wait_recv()
-            self.xc = []
+        if s == 1 and self.order == "xy":
             for d in range(1, X):
                 to = p.to("x", d)
 
                 def one(at, to=to, d=d):
-                    mine = self.full[pl.ds(pl.multiple_of(self.rows_of(to, p.k) + at, 16), 16), :]
-                    self.xs[d - 1, pl.ds(at, 16), :] = (mine + self.cr[to, pl.ds(at, 16), :]).astype(bf16)
+                    self.xs[d - 1, 0, pl.ds(at, 16), :] = self.sum_core(to, at).astype(bf16)
 
                 by_rows(self.shard, 16, one)
-                self.xc.append(self._send(X + d - 1, self.xs.at[d - 1], self.xr.at[d - 1], p.peer("x", d)))
-        elif s == 2:
-            for copy in self.xc:
-                copy.wait_recv()
-
-            def total(at, n=16):
-                value = self.full[pl.ds(pl.multiple_of(self.rows_of(p.x, p.k) + at, 16), n), :]
-                value = value + self.cr[p.x, pl.ds(at, n), :]
-                for d in range(1, X):
-                    value = value + self.xr[d - 1, pl.ds(at, n), :].astype(f32)
-                return value
-
-            self.yc = []
+        elif s == 1:
             for d in range(1, Y):
                 base = p.to("y", d) * self.ry
 
                 def one(at, base=base, d=d):
-                    self.ys[d - 1, pl.ds(at, 16), :] = total(pl.multiple_of(base + at, 16)).astype(bf16)
+                    for x in range(X):
+                        self.ys[d - 1, x, pl.ds(at, 16), :] = self.sum_core(x, pl.multiple_of(base + at, 16)).astype(bf16)
 
                 by_rows(self.ry, 16, one)
-                self.yc.append(self._send(2 * X - 2 + d, self.ys.at[d - 1], self.yr.at[d - 1], p.peer("y", d)))
+        elif s == 2:
+            if self.order == "xy":
+                for d in range(1, Y):
+
+                    def one(at, to=p.to("y", d), d=d):
+                        self.ys[d - 1, 0, pl.ds(at, 16), :] = self.sum_first(p.x, to, at).astype(bf16)
+
+                    by_rows(self.ry, 16, one)
+            else:
+                for d in range(1, X):
+
+                    def one(at, to=p.to("x", d), d=d):
+                        self.xs[d - 1, 0, pl.ds(at, 16), :] = self.sum_first(to, p.y, at).astype(bf16)
+
+                    by_rows(self.ry, 16, one)
 
             def mine(at):
-                at = pl.multiple_of(p.y * self.ry + at, 16)
-                self.cr[p.x, pl.ds(at, 16), :] = total(at)
+                self.cr[p.x, pl.ds(pl.multiple_of(p.y * self.ry + at, 16), 16), :] = self.sum_first(p.x, p.y, at)
 
             by_rows(self.ry, 16, mine)
         elif s == 3:
-            for copy in self.yc:
-                copy.wait_recv()
 
             def total(z):
-                rows, lanes = self.piece_at(z)
-                value = self.cr[p.x, pl.ds(pl.multiple_of(p.y * self.ry + rows, 16), self.rz), lanes]
-                for d in range(1, Y):
-                    value = value + self.yr[d - 1, pl.ds(rows, self.rz), lanes].astype(f32)
+                rows = pl.multiple_of(z * self.rz, 16)
+                value = self.cr[p.x, pl.ds(pl.multiple_of(p.y * self.ry + rows, 16), self.rz), :]
+                arrived = self.yr if self.order == "xy" else self.xr
+                for d in range(1, Y if self.order == "xy" else X):
+                    value = value + arrived[d - 1, 0, pl.ds(rows, self.rz), :].astype(f32)
                 return value
 
-            self.zc = []
-            base = 2 * X - 1 + Y - 1
             for d in range(1, Z):
                 self.zs[d - 1] = total(p.to("z", d)).astype(self.late)
-                self.zc.append(self._send(base + d - 1, self.zs.at[d - 1], self.zin.at[d - 1], p.peer("z", d)))
             self.piece[...] = total(p.z)
         elif s == 4:
-            for copy in self.zc:
-                copy.wait_recv()
             value = self.piece[...]
             for d in range(1, Z):
                 value = value + self.zin[d - 1].astype(f32)
             self.piece[...] = value
-            rows, lanes = self.piece_at(p.z)
-            here = self.out.at[pl.ds(pl.multiple_of(p.y * self.ry + rows, 16), self.rz), lanes]
-            here[...] = value.astype(self.late)
-            base = 2 * X - 1 + Y - 1 + Z - 1
-            self.gz = [self._send(base + d - 1, here, here, p.peer("z", d)) for d in range(1, Z)]
-        elif s == 5:
-            for copy in self.gz:
-                copy.wait_recv()
-            here = self.out.at[pl.ds(pl.multiple_of(p.y * self.ry, 16), self.ry), :]
-            base = 2 * X - 1 + Y - 1 + 2 * (Z - 1)
-            self.gy = [self._send(base + d - 1, here, here, p.peer("y", d)) for d in range(1, Y)]
-        elif s == 6:
-            for copy in self.gy:
-                copy.wait_recv()
+            self.out[self.place_z(), :] = value.astype(self.late)
+        if s < STAGES - 1:
+            for copy in self.copies(s):
+                copy.start()
 
     def drain(self):
-        for copy in self.copies:
-            copy.wait_send()
+        for s in range(1 if self.lent else 0, STAGES - 1):
+            for copy in self.copies(s):
+                copy.wait_send()
 
 
 STAGES = 7
@@ -352,13 +365,16 @@
         self.N = MESH_DEV
         self.SH = dim // self.n_col
         self.R, self.Q = self.n_row * self.N, self.n_col * self.N
-        chunk = lambda width, late: Reduce(self.grid, dim, self.n_col, width, late)
+        chunk = functools.partial(Reduce, self.grid, dim, self.n_col)
+        skips, decoders = chunk(dim + N_OUT, f32, "xy"), chunk(2 * dim, bf16, "xy")
+        skips.lent = decoders.lent = True
         self.chunks = [
-            chunk(dim + N_OUT, f32),
-            chunk(2 * dim, bf16),
-            chunk(2 * dim, bf16),
-            chunk(dim, bf16),
-            chunk(N_IN, f32),
+            skips,
+            decoders,
+            chunk(dim, bf16, "xy", decoders, 0),
+            chunk(dim, bf16, "xy", decoders, dim),
+            chunk(dim, bf16, "yx", skips, 0),
+            chunk(N_IN, f32, "yx"),
         ]
         X, Y, Z = self.grid
         S, C, D, E, N, R, Q = self.S, self.C, self.D, self.E, self.N, self.R, self.Q
@@ -422,11 +438,15 @@
             px_rs=dma(2, S, X - 1),
             a_ss=dma(S, 1 + 2 * (X - 1)),
             a_rs=dma(S, 1 + 2 * (X - 1)),
-            dy_ss=dma(S, Y - 1),
-            dy_rs=dma(S, Y - 1),
+            dy_ss=dma(S, Y - 1, Z),
+            dy_rs=dma(S, Y - 1, Z),
             dz_ss=dma(S, Z - 1),
             dz_rs=dma(S, Z - 1),
         )
+
+    def fits(self):
+        X, Y, Z = self.grid
+        return self.SH % (16 * Y * Z) == 0 and self.SH % 128 == 0 and self.vmem_bytes() < VMEM_ROOM
 
     def vmem_bytes(self):
         total = 0
@@ -441,7 +461,7 @@
 
     def scratch(self):
         total = Total.scratch(*self.grid)
-        return [*self.shapes.values(), *total * 3, *[s for c in self.chunks for s in c.scratch()]]
+        return [*self.shapes.values(), *total * 2, *[s for c in self.chunks for s in c.scratch()]]
 
     def kernel(self, count, x, tgt, area, node, snd, rcv, wi, wl, wo, mi, mal, mo, si, sal, so, *refs):
         S, C, D, E, N, R, Q, SH = self.S, self.C, self.D, self.E, self.N, self.R, self.Q, self.SH
@@ -450,8 +470,8 @@
         v = types.SimpleNamespace(**dict(zip(self.shapes, refs)))
         refs = refs[len(self.shapes) :]
         p = Place(self.n_row, self.n_col)
-        area_sum, loss_sum, norm_sum = (Total(p, refs[i : i + 7]) for i in (0, 7, 14))
-        refs = refs[21:]
+        area_sum, stat_sum = Total(p, refs[:7]), Total(p, refs[7:14])
+        refs = refs[14:]
         for chunk in self.chunks:
             many = len(chunk.scratch())
             chunk.bind(p, refs[:many])
@@ -481,7 +501,11 @@
                 w_copy(i, 2, d).wait_recv()
 
         W = lambda which: v.wlb[which]
+        barrier = p.greet()
         own = ds(p.col * SH, SH)
+        loads = [pltpu.make_async_copy(wl.at[m], v.fp.at[m * SH : (m + 1) * SH, :], v.l_sem.at[m]) for m in range(6)]
+        for load in loads:
+            load.start()
 
         def turned(ref, n):
             v.tmp[0:n, 0:SH] = jnp.zeros((n, SH), f32)
@@ -489,20 +513,25 @@
             return jnp.transpose(v.tmp[0:n, 0:SH])
 
         v.wib[own, :] = turned(wi, N_IN).astype(bf16)
-        loads = [pltpu.make_async_copy(wl.at[m], v.fp.at[m * SH : (m + 1) * SH, :], v.l_sem.at[m]) for m in range(6)]
-        for load in loads:
-            load.start()
+        v.wob[own, :] = turned(wo, N_OUT).astype(bf16)
         for m, load in enumerate(loads):
             load.wait()
             v.wlb[m, own, :] = v.fp[m * SH : (m + 1) * SH, :].astype(bf16)
-        v.wob[own, :] = turned(wo, N_OUT).astype(bf16)
-        p.barrier()
-        for i in range(8):
-            w_copy(i, 0).start()
-            for d in hops:
-                w_copy(i, 1, d).start()
-
         used = count[0]
+        area_row = area[...].reshape(1, C) * (lax.broadcasted_iota(jnp.int32, (1, C), 1) < used).astype(f32)
+        area_sum.value[...] = jnp.broadcast_to(jnp.sum(area_row), (8, 128))
+        pl.semaphore_wait(*barrier)
+
+
+        def w_depart(*items):
+            for i in items:
+                w_copy(i, 0).start()
+                for d in hops:
+                    w_copy(i, 1, d).start()
+
+        w_depart(0, 1, 2, 3)
+        area_sum.start("y")
+
         node_row = node[...].reshape(1, C)
         match = (lax.broadcasted_iota(jnp.int32, (N, C), 0) == node_row).astype(f32)
         v.nm[...] = match.astype(bf16)
@@ -510,14 +539,27 @@
         v.nv[...] = match.astype(bf16)
         v.cnt[...] = jnp.broadcast_to(jnp.maximum(jnp.sum(match, axis=1, keepdims=True), 1.0), (N, 128))
         node_col = jnp.transpose(jnp.broadcast_to(node_row, (128, C)))
-        area_row = area[...].reshape(1, C) * (lax.broadcasted_iota(jnp.int32, (1, C), 1) < used).astype(f32)
         v.cw[...] = jnp.transpose(jnp.broadcast_to(area_row, (128, C)))
         match = (lax.broadcasted_iota(jnp.int32, (C, 128), 1) == node_col).astype(f32)
         v.cm[...] = match[:, :N].astype(bf16)
         match = match * (lax.broadcasted_iota(jnp.int32, (C, 128), 0) < used).astype(f32)
         v.cmv[...] = match[:, :N].astype(bf16)
-        area_sum.value[...] = jnp.broadcast_to(jnp.sum(area_row), (8, 128))
-        area_sum.start("k")
+
+        def table(index, base, rows):
+            def down(at):
+                hit = lax.broadcasted_iota(jnp.int32, (128, E), 0) + at == index
+                v.oht[pl.ds(pl.multiple_of(base + at, 128), 128), :] = hit.astype(f32).astype(bf16)
+
+            by_rows(rows, 128, down)
+            column = jnp.transpose(jnp.broadcast_to(index, (128, E)))
+            for at in range(0, rows, 128):
+                hit = lax.broadcasted_iota(jnp.int32, (E, 128), 1) + at == column
+                v.oh[:, base + at : base + at + 128] = hit.astype(f32).astype(bf16)
+
+        table(snd[...], 0, R)
+        table(rcv[...], R, Q)
+        v.dp[...] = jnp.zeros((S * C, N_OUT), bf16)
+        v.loss[...] = jnp.zeros((8, 128), f32)
 
         w_forward(0)
         w_get(0)
@@ -532,20 +574,13 @@
             return carry
 
         lax.fori_loop(0, S, encode, 0)
-        area_sum.finish("k")
-        area_sum.start("x")
+        area_sum.finish("y")
+        area_sum.start("z")
         w_forward(1)
         w_get(1)
         pre = mm(v.av[...], W(0))
         v.sp[...] = pre
         v.mlb[...] = silu(pre).astype(bf16)
-        w_forward(2)
-        w_get(2)
-        v.tmp[0 : S * N, :] = mm(v.mlb[...], W(1))
-        for s in range(S):
-            v.sr[s, ds(p.row * N, N), :] = v.tmp[s * N : (s + 1) * N, :].astype(bf16)
-        w_forward(3)
-        w_get(3)
 
         def mz(s, d):
             rows = v.sr.at[s, ds(p.row * N, N), :]
@@ -562,44 +597,33 @@
             return remote(rows, rows, v.mr_ss.at[s, at], v.mr_rs.at[s, at], p.peer("x", d) if j == 1 else p.peer("k", 1))
 
         for s in range(S):
+            v.sr[s, ds(p.row * N, N), :] = v.mlb[s * N : (s + 1) * N, :]
+            v.sr[s, ds(R + p.col * N, N), :] = v.mlb[s * N : (s + 1) * N, :]
+
+        def depart(s):
             for d in range(1, Z):
                 mz(s, d).start()
+
+        depart(0)
+        for s in range(S):
             for d in range(1, Y):
                 my(s, d, 0).start()
-        v.tmp[0 : S * N, :] = mm(v.mlb[...], W(2))
-        for s in range(S):
-            v.sr[s, ds(R + p.col * N, N), :] = v.tmp[s * N : (s + 1) * N, :].astype(bf16)
-        for s in range(S):
             mr(s, 0).start()
             for d in hops:
                 mr(s, 1, d).start()
-        area_sum.finish("x")
-        area_sum.start("y")
-
-        def table(index, base, rows):
-            def down(at):
-                hit = lax.broadcasted_iota(jnp.int32, (128, E), 0) + at == index
-                v.oht[pl.ds(pl.multiple_of(base + at, 128), 128), :] = hit.astype(f32).astype(bf16)
-
-            by_rows(rows, 128, down)
-            column = jnp.transpose(jnp.broadcast_to(index, (128, E)))
-            for at in range(0, rows, 128):
-                hit = lax.broadcasted_iota(jnp.int32, (E, 128), 1) + at == column
-                v.oh[:, base + at : base + at + 128] = hit.astype(f32).astype(bf16)
-
-        table(snd[...], 0, R)
-        table(rcv[...], R, Q)
-
-        w_forward(4)
-        w_get(4)
+            if s == 1:
+                w_depart(4)
+        w_depart(5, 6, 7)
+        w_forward(2)
+        w_forward(3)
+        depart(1)
+        area_sum.finish("z")
+        area_sum.start("x")
+        w_get(2)
+        w_get(3)
 
         def skip(at):
             v.tp[pl.ds(at, 512), :] = mm(v.gl[pl.ds(at, 512), :], W(5))
-
-        by_rows(S * C, 512, skip)
-        area_sum.finish("y")
-        area_sum.start("z")
-        w_forward(5)
 
         def pk(t, s, xx):
             rows = v.part.at[s, ds((2 * xx + 1 - p.k) * N, N), :]
@@ -624,8 +648,18 @@
                 total = total + v.pxr[s, d - 1].astype(f32)
             return total
 
+        def nearest(j):
+            steps = [(n + 1) // 2 * (1 if n % 2 else -1) for n in range(1, 2 * Z - 1)]
+            taken, found = jnp.int32(0), jnp.int32(0)
+            for step in steps:
+                inside = ((p.z - step >= 0) & (p.z - step < Z)).astype(jnp.int32)
+                found = found + jnp.where((taken == j) & (inside == 1), step, 0)
+                taken = taken + inside
+            return (found + Z) % Z
+
         def arrive(s):
-            for d in range(1, Z):
+            for j in range(Z - 1):
+                d = nearest(j)
                 mz(s, d).wait_recv()
                 for b in range(1, Y):
                     my(s, b, d).start()
@@ -640,6 +674,17 @@
             mr(s, 0).wait_recv()
             for d in hops:
                 mr(s, 2, d).wait_recv()
+            for d in range(1, Z):
+                mz(s, d).wait_send()
+            for b in range(1, Y):
+                for e in range(Z):
+                    my(s, b, e).wait_send()
+            mr(s, 0).wait_send()
+            for d in hops:
+                mr(s, 1, d).wait_send()
+                mr(s, 2, d).wait_send()
+            v.sr[s, 0:R, :] = mm(v.sr[s, 0:R, :], W(1)).astype(bf16)
+            v.sr[s, R : R + Q, :] = mm(v.sr[s, R : R + Q, :], W(2)).astype(bf16)
 
             def pick(at):
                 pre = mm(v.oh[pl.ds(at, 512), :], v.sr[s])
@@ -651,38 +696,17 @@
             for xx in range(X):
                 pk(0, s, xx).start()
 
-        def forward(i, carry):
-            @pl.when(i < S)
-            def _():
-                arrive(i)
-
-            @pl.when((i >= 1) & (i <= S))
-            def _():
-                edges(i - 1)
-
-            @pl.when(i >= 2)
-            def _():
-                col_second(0, i - 2)
-
-            return carry
-
-        lax.fori_loop(0, S + 2, forward, 0)
-        area_sum.finish("z")
-        w_get(5)
-        for i in (6, 7):
-            w_forward(i)
-        for s in range(S):
-            v.agb[s * N : (s + 1) * N, :] = (col_last(0, s) * (1.0 / DEG)).astype(bf16)
-
-        v.mnb[...] = (silu(v.sp[...]) + mm(v.agb[...], W(3))).astype(bf16)
-        w_get(6)
-        w_get(7)
-        v.dp[...] = jnp.zeros((S * C, N_OUT), bf16)
-        v.loss[...] = jnp.zeros((8, 128), f32)
-        scale = 1.0 / (C_OUT * S * area_sum.value[0:1, 0:1])
-
-        def decode(s, carry):
+        def ac(s, j, d=0):
+            col = 2 * p.to("x", -d) + p.k if j == 2 else p.col
+            rows = v.da.at[s, ds(col * N, N), :]
+            at = (0, d, X - 1 + d)[j]
+            return remote(rows, rows, v.a_ss.at[s, at], v.a_rs.at[s, at], p.peer("x", d) if j == 1 else p.peer("k", 1))
+
+        def decode(s):
             at, here = ds(s * C, C), ds(s * N, N)
+            v.agb[here, :] = (col_last(0, s) * (1.0 / DEG)).astype(bf16)
+            v.mnb[here, :] = (silu(v.sp[here, :]) + mm(v.agb[here, :], W(3))).astype(bf16)
+            scale = 1.0 / (C_OUT * S * area_sum.value[0:1, 0:1])
             rows = mm(v.cm[...], v.mnb[here, :]).astype(bf16)
             pre = mm(rows, W(4)) + v.tp[at, :]
             v.tp[at, :] = pre
@@ -692,49 +716,18 @@
             v.loss[0:1, 0:C_OUT] = v.loss[0:1, 0:C_OUT] + jnp.sum(weighted * error, axis=0, keepdims=True)
             v.dp[at, 0:C_OUT] = (2.0 * weighted * scale).astype(bf16)
             v.dt[at, :] = (silu_slope(v.tp[at, :]) * mm_nt(v.dp[at, :], v.wob[...])).astype(bf16)
-            v.sg[here, :] = mm(v.nm[...], v.dt[at, :])
-            return carry
-
-        lax.fori_loop(0, S, decode, 0)
-        high, low = high_low(v.sg[...])
-        v.dmn[...] = mm_nt(high, W(4)) + mm_nt(low, W(4))
-        v.tmp[0 : S * N, :] = mm_nt(v.dmn[...].astype(bf16), W(3))
-        for s in range(S):
-            v.da[s, ds(p.col * N, N), :] = v.tmp[s * N : (s + 1) * N, :].astype(bf16)
-
-        def ac(s, j, d=0):
-            col = 2 * p.to("x", -d) + p.k if j == 2 else p.col
-            rows = v.da.at[s, ds(col * N, N), :]
-            at = (0, d, X - 1 + d)[j]
-            return remote(rows, rows, v.a_ss.at[s, at], v.a_rs.at[s, at], p.peer("x", d) if j == 1 else p.peer("k", 1))
-
-        for s in range(S):
+            grad = mm(v.nm[...], v.dt[at, :])
+            v.sg[here, :] = grad
+            grad = mm_nt(jnp.concatenate(high_low(grad), axis=0), W(4))
+            grad = grad[:N] + grad[N:]
+            v.dmn[here, :] = grad
+            v.da[s, ds(p.col * N, N), :] = mm_nt(grad.astype(bf16), W(3)).astype(bf16)
             ac(s, 0).start()
             for d in hops:
                 ac(s, 1, d).start()
-        loss_sum.value[...] = jnp.broadcast_to(jnp.sum(v.loss[...]), (8, 128))
-        loss_sum.start("k")
-
-        first, second, third, fourth, fifth = self.chunks
-        first.full[:, 0:D] = mm_tn(v.gl[...], v.dt[...])
-        first.full[:, D : D + N_OUT] = mm_tn(v.go[...], v.dp[...])
-        first.stage(0)
-        high, low = high_low(v.sg[...])
-        second.full[:, 0:D] = mm_tn(v.mnb[...], high) + mm_tn(v.mnb[...], low)
-        second.full[:, D : 2 * D] = mm_tn(v.agb[...], v.dmn[...].astype(bf16))
-        second.stage(0)
-
-        def skip_back(at):
-            v.tp[pl.ds(at, 512), :] = mm_nt(v.dt[pl.ds(at, 512), :], W(5))
-
-        by_rows(S * C, 512, skip_back)
-        loss_sum.finish("k")
-        loss_sum.start("x")
-        first.stage(1)
-        second.stage(1)
-
-        def dy(s, d):
-            return remote(v.dys.at[s, d - 1], v.dyr.at[s, d - 1], v.dy_ss.at[s, d - 1], v.dy_rs.at[s, d - 1], p.peer("y", d))
+
+        def dy(s, d, e):
+            return remote(v.dys.at[s, d - 1, e], v.dyr.at[s, d - 1, e], v.dy_ss.at[s, d - 1, e], v.dy_rs.at[s, d - 1, e], p.peer("y", d))
 
         def dz(s, d):
             return remote(v.dzs.at[s, d - 1], v.dzr.at[s, d - 1], v.dz_ss.at[s, d - 1], v.dz_rs.at[s, d - 1], p.peer("z", d))
@@ -748,6 +741,10 @@
             ac(s, 0).wait_recv()
             for d in hops:
                 ac(s, 2, d).wait_recv()
+            for xx in range(X):
+                pk(0, s, xx).wait_send()
+            for d in hops:
+                px(0, s, d).wait_send()
 
             def pick(at):
                 grad = mm(v.oh[pl.ds(at, 512), R:], v.da[s])
@@ -755,51 +752,108 @@
 
             by_rows(E, 512, pick)
             v.tmp[...] = mm(v.oht[...], v.ac[...])
-            for d in range(1, Y):
-                for e in range(Z):
-                    v.dys[s, d - 1, e] = v.tmp[ds((e * Y + p.to("y", d)) * N, N), :].astype(bf16)
-                dy(s, d).start()
-            for e in range(Z):
-                v.down[s, e] = v.tmp[ds((e * Y + p.y) * N, N), :]
+            for e in (*range(1, Z), 0):
+                to = p.to("z", e)
+                for d in range(1, Y):
+                    v.dys[s, d - 1, e] = v.tmp[ds((to * Y + p.to("y", d)) * N, N), :].astype(bf16)
+                    dy(s, d, e).start()
+                v.down[s, e] = v.tmp[ds((to * Y + p.y) * N, N), :]
             v.part[s] = v.tmp[R:, :]
             for xx in range(X):
                 pk(1, s, xx).start()
 
+        def row_sum(s, e):
+            total = v.down[s, e]
+            for d in range(1, Y):
+                dy(s, d, e).wait_recv()
+                total = total + v.dyr[s, d - 1, e].astype(f32)
+            return total
+
         def row_second(s):
-            for d in range(1, Y):
-                dy(s, d).wait_recv()
-
-            def summed(e):
-                total = v.down[s, e]
-                for d in range(1, Y):
-                    total = total + v.dyr[s, d - 1, e].astype(f32)
-                return total
-
+            for e in range(1, Z):
+                v.dzs[s, e - 1] = row_sum(s, e).astype(bf16)
+                dz(s, e).start()
+
+        def encode_back(s):
+            at, here = ds(s * C, C), ds(s * N, N)
+            v.drb[here, :] = col_last(1, s).astype(bf16)
+            total = row_sum(s, 0)
             for d in range(1, Z):
-                v.dzs[s, d - 1] = summed(p.to("z", d)).astype(bf16)
-                dz(s, d).start()
-            v.down[s, p.z] = summed(p.z)
-
-        for s in range(S):
-            for xx in range(X):
-                pk(0, s, xx).wait_send()
-            for d in hops:
-                px(0, s, d).wait_send()
-
-        def backward(i, carry):
-            @pl.when(i < S)
-            def _():
-                pass_on(i)
-                edges_back(i)
-
-            @pl.when(i >= 1)
-            def _():
-                col_second(1, i - 1)
-                row_second(i - 1)
-
+                dz(s, d).wait_recv()
+                total = total + v.dzr[s, d - 1].astype(f32)
+            v.dsb[here, :] = total.astype(bf16)
+            whole = v.dmn[here, :] + mm_nt(v.dsb[here, :], W(1)) + mm_nt(v.drb[here, :], W(2))
+            v.d2b[here, :] = (silu_slope(v.sp[here, :]) * whole).astype(bf16)
+            high, low = high_low(mm_nt(v.d2b[here, :], W(0)) / v.cnt[:, 0:1])
+            grad = v.tp[at, :] + mm(v.cmv[...], high) + mm(v.cmv[...], low)
+            v.dt[at, :] = (silu_slope(v.fp[at, :]) * grad).astype(bf16)
+
+        skips, decoders, senders, receivers, encoders, inputs = self.chunks
+
+        def decoder_gradients():
+            skips.full[:, 0:D] = mm_tn(v.gl[...], v.dt[...])
+            skips.full[:, D : D + N_OUT] = mm_tn(v.go[...], v.dp[...])
+            skips.stage(0)
+            high, low = high_low(v.sg[...])
+            decoders.full[:, 0:D] = mm_tn(v.mnb[...], high) + mm_tn(v.mnb[...], low)
+            decoders.full[:, D : 2 * D] = mm_tn(v.agb[...], v.dmn[...].astype(bf16))
+            decoders.stage(0)
+
+        def skip_back():
+            def one(at):
+                v.tp[pl.ds(at, 512), :] = mm_nt(v.dt[pl.ds(at, 512), :], W(5))
+
+            by_rows(S * C, 512, one)
+
+        def weights_rest():
+            for i in (5, 6, 7):
+                w_forward(i)
+            area_sum.finish("x")
+            area_sum.start("k")
+            for i in (5, 6, 7):
+                w_get(i)
+            area_sum.finish("k")
+
+        def partials_back(s):
+            col_second(1, s)
+            row_second(s)
+
+        stage = lambda chunk, n: functools.partial(chunk.stage, n)
+        line = [
+            (edges_back, 3),
+            (stage(decoders, 1), S + 2, None),
+            (edges, 0),
+            (arrive, -2),
+            (weights_rest, 1, None),
+            (decoder_gradients, S + 1, None),
+            (partials_back, 4),
+            (pass_on, 2),
+            (stage(skips, 1), S + 1, None),
+            (skip_back, S + 2, None),
+            (decode, 1),
+            (functools.partial(col_second, 0), 0),
+            (stage(skips, 3), S + 5, None),
+            (encode_back, 6),
+            (stage(skips, 2), S + 3, None),
+            (stage(decoders, 2), S + 3, None),
+        ]
+        arrive(0)
+        depart(2)
+        w_forward(4)
+        w_get(4)
+        by_rows(S * C, 512, skip)
+        arrive(1)
+        depart(3)
+
+        def turn(i, carry):
+            for todo, behind, *once in line:
+                if once:
+                    pl.when(i == behind)(todo)
+                else:
+                    pl.when((i >= max(behind, 0)) & (i < S + behind))(functools.partial(todo, i - behind))
             return carry
 
-        lax.fori_loop(0, S + 1, backward, 0)
+        lax.fori_loop(0, S + 6, turn, 0)
         states = [
             pltpu.make_async_copy(a.at[m], v.ep.at[j, m * SH : (m + 1) * SH, :], v.l_sem.at[6 + 6 * j + m])
             for j, a in enumerate((wl, mal, sal))
@@ -807,106 +861,97 @@
         ]
         for load in states:
             load.start()
-        first.stage(2)
-        second.stage(2)
-        for s in range(S):
-            v.drb[s * N : (s + 1) * N, :] = col_last(1, s).astype(bf16)
-        for s in range(S):
-            total = v.down[s, p.z]
-            for d in range(1, Z):
-                dz(s, d).wait_recv()
-                total = total + v.dzr[s, d - 1].astype(f32)
-            v.dsb[s * N : (s + 1) * N, :] = total.astype(bf16)
-
-        third.full[:, 0:D] = mm_tn(v.mlb[...], v.dsb[...])
-        third.full[:, D : 2 * D] = mm_tn(v.mlb[...], v.drb[...])
-        third.stage(0)
-        whole = v.dmn[...] + mm_nt(v.dsb[...], W(1)) + mm_nt(v.drb[...], W(2))
-        v.d2b[...] = (silu_slope(v.sp[...]) * whole).astype(bf16)
-        third.stage(1)
-        fourth.full[...] = mm_tn(v.av[...], v.d2b[...])
-        fourth.stage(0)
-        v.dmn[...] = mm_nt(v.d2b[...], W(0))
-        first.stage(3)
-        second.stage(3)
-
-        def encode_back(s, carry):
-            at, here = ds(s * C, C), ds(s * N, N)
-            high, low = high_low(v.dmn[here, :] / v.cnt[:, 0:1])
-            grad = v.tp[at, :] + mm(v.cmv[...], high) + mm(v.cmv[...], low)
-            v.dt[at, :] = (silu_slope(v.fp[at, :]) * grad).astype(bf16)
-            return carry
-
-        lax.fori_loop(0, S, encode_back, 0)
-        third.stage(2)
-        fourth.stage(1)
-        fifth.full[:, self.c_in :] = jnp.zeros((D, N_IN - self.c_in), f32)
+        decoders.lend()
+        skips.lend()
+        senders.full[...] = mm_tn(v.mlb[...], v.dsb[...])
+        senders.stage(0)
+        receivers.full[...] = mm_tn(v.mlb[...], v.drb[...])
+        receivers.stage(0)
+        encoders.full[...] = mm_tn(v.av[...], v.d2b[...])
+        encoders.stage(0)
+        inputs.full[:, self.c_in :] = jnp.zeros((D, N_IN - self.c_in), f32)
         for s in range(S):
             grad = mm_tn(v.dt[s * C : (s + 1) * C, :], x[s])
             if s:
-                grad = grad + fifth.full[:, : self.c_in]
-            fifth.full[:, : self.c_in] = grad
-        fifth.stage(0)
-        first.stage(4)
-        second.stage(4)
-        loss_sum.finish("x")
-        loss_sum.start("y")
-        third.stage(3)
-        fourth.stage(2)
-        fifth.stage(1)
-        first.stage(5)
-        second.stage(5)
-        third.stage(4)
-        fourth.stage(3)
-        fifth.stage(2)
-        loss_sum.finish("y")
-        loss_sum.start("z")
+                grad = grad + inputs.full[:, : self.c_in]
+            inputs.full[:, : self.c_in] = grad
+        inputs.stage(0)
+        senders.stage(1)
+        encoders.stage(1)
+        receivers.stage(1)
+        inputs.stage(1)
+        decoders.stage(3)
+
         for load in states:
             load.wait()
+        spare = v.ep.at[3]
+        for j, (a, b) in enumerate(((wi, wo), (mi, mo), (si, so))):
+            spare[j * SH : (j + 1) * SH, 0:N_IN] = turned(a, N_IN)
+            spare[j * SH : (j + 1) * SH, N_IN : N_IN + N_OUT] = turned(b, N_OUT)
         lane = lax.broadcasted_iota(jnp.int32, (8, 128), 1)
         row = lax.broadcasted_iota(jnp.int32, (8, 128), 0)
-        norm_sum.value[...] = jnp.zeros((8, 128), f32)
-
-        def note(j, weight, gradient, mean, square):
-            _, _, update = adam_parts(weight, gradient, mean, square)
-            for i, what in enumerate((weight, update)):
-                norm_sum.value[...] += jnp.where((row == i) & (lane == j), jnp.sum(what * what), 0.0)
+        stat_sum.value[...] = jnp.where(row == 2, jnp.sum(v.loss[...]), 0.0)
+
+        def note(j, gradient, at, lanes):
+            held = [buf[pl.ds(pl.multiple_of(start + p.y * (SH // Y) + p.z * (SH // Y // Z), 16), SH // Y // Z), lanes] for buf, start in at]
+            _, _, update = adam_parts(held[0], gradient, held[1], held[2])
+            for i, what in enumerate((held[0], update)):
+                stat_sum.value[...] += jnp.where((row == i) & (lane == j), jnp.sum(what * what), 0.0)
 
         def note_latent(m, gradient):
-            weight, mean, square = (v.ep[j, m * SH : (m + 1) * SH, :] for j in range(3))
-            note(1 + m, weight, gradient.astype(f32), mean, square)
-
-        first.stage(6)
-        g_skip[...] = first.out[:, :D]
-        g_out[...] = jnp.transpose(first.out[:, D : D + N_OUT])[: g_out.shape[0], :]
-        second.stage(6)
-        g_two[...] = second.out[:, : 2 * D]
-        third.stage(5)
-        fourth.stage(4)
-        fifth.stage(3)
-        note_latent(5, first.out[:, :D])
-        note(7, wo[...], g_out[...], mo[...], so[...])
-        note_latent(4, second.out[:, 0:D])
-        note_latent(3, second.out[:, D : 2 * D])
-        third.stage(6)
-        g_three[...] = third.out[:, : 2 * D]
-        fourth.stage(5)
-        fifth.stage(4)
-        note_latent(1, third.out[:, 0:D])
-        note_latent(2, third.out[:, D : 2 * D])
-        fourth.stage(6)
-        g_four[...] = fourth.out[:, :D]
-        fifth.stage(5)
-        note_latent(0, fourth.out[:, :D])
-        loss_sum.finish("z")
-        fifth.stage(6)
-        g_in[...] = jnp.transpose(fifth.out[:, :N_IN])[: g_in.shape[0], :]
-        note(0, wi[...], g_in[...], mi[...], si[...])
-        norm_sum.start("k")
-        norm_sum.finish("k")
-        norm_sum.start("x")
-        norm_sum.finish("x")
-        stats[...] = jnp.where(row < 2, norm_sum.value[...], loss_sum.value[...] / (C_OUT * S * area_sum.value[...]))
+            note(1 + m, gradient, [(v.ep.at[j], m * SH) for j in range(3)], slice(None))
+
+        edge = [(spare, j * SH) for j in range(3)]
+        skips.stage(4)
+        note_latent(5, skips.piece[:, 0:D])
+        note(7, skips.piece[:, D : D + N_OUT], edge, slice(N_IN, N_IN + N_OUT))
+        senders.stage(2)
+        encoders.stage(2)
+        decoders.stage(4)
+        note_latent(4, decoders.piece[:, 0:D])
+        note_latent(3, decoders.piece[:, D : 2 * D])
+        receivers.stage(2)
+        inputs.stage(2)
+        skips.stage(5)
+        senders.stage(3)
+        encoders.stage(3)
+        receivers.stage(3)
+        inputs.stage(3)
+        decoders.stage(5)
+        senders.stage(4)
+        note_latent(1, senders.piece[...])
+        encoders.stage(4)
+        note_latent(0, encoders.piece[...])
+        receivers.stage(4)
+        note_latent(2, receivers.piece[...])
+        inputs.stage(4)
+        note(0, inputs.piece[...], edge, slice(0, N_IN))
+        stat_sum.start("k")
+        skips.stage(6)
+        g_skip[...] = skips.out[:, :D]
+        g_out[...] = jnp.transpose(skips.out[:, D : D + N_OUT])[: g_out.shape[0], :]
+        stat_sum.finish("k")
+        stat_sum.start("x")
+        decoders.stage(6)
+        g_two[...] = decoders.out[...]
+        senders.stage(5)
+        encoders.stage(5)
+        stat_sum.finish("x")
+        stat_sum.start("z")
+        receivers.stage(5)
+        inputs.stage(5)
+        senders.stage(6)
+        g_three[:, 0:D] = senders.out[...]
+        encoders.stage(6)
+        g_four[...] = encoders.out[...]
+        stat_sum.finish("z")
+        stat_sum.start("y")
+        receivers.stage(6)
+        g_three[:, D : 2 * D] = receivers.out[...]
+        inputs.stage(6)
+        g_in[...] = jnp.transpose(inputs.out[...])[: g_in.shape[0], :]
+        stat_sum.finish("y")
+        stats[...] = jnp.where(row < 2, stat_sum.value[...], stat_sum.value[...] / (C_OUT * S * area_sum.value[...]))
 
         for i in range(8):
             w_copy(i, 0).wait_send()
@@ -915,24 +960,20 @@
                 w_copy(i, 2, d).wait_send()
         for s in range(S):
             for d in range(1, Z):
-                mz(s, d).wait_send()
                 dz(s, d).wait_send()
             for d in range(1, Y):
                 for e in range(Z):
-                    my(s, d, e).wait_send()
-                dy(s, d).wait_send()
-            for copy in (mr, ac):
-                copy(s, 0).wait_send()
-                for d in hops:
-                    copy(s, 1, d).wait_send()
-                    copy(s, 2, d).wait_send()
+                    dy(s, d, e).wait_send()
+            ac(s, 0).wait_send()
+            for d in hops:
+                ac(s, 1, d).wait_send()
+                ac(s, 2, d).wait_send()
             for xx in range(X):
                 pk(1, s, xx).wait_send()
             for d in hops:
                 px(1, s, d).wait_send()
         area_sum.drain("kxyz")
-        loss_sum.drain("kxyz")
-        norm_sum.drain("kx")
+        stat_sum.drain("kxyz")
         for chunk in self.chunks:
             chunk.drain()
 
@@ -1177,7 +1218,7 @@
     given = (inputs, targets, cell_area, cell_count, cell_node, edge_senders, edge_receivers, weight_input, weight_latent, weight_output)
     states = (mean_input, mean_latent, mean_output, square_input, square_latent, square_output)
     step = Step(mesh, inputs.shape[0], inputs.shape[1], weight_latent.shape[2], edge_senders.shape[0], inputs.shape[2])
-    if step.vmem_bytes() < VMEM_ROOM:
+    if step.fits():
         return kernel_body(mesh, step, *given, *states)
     loss_value, gradient_input, gradient_latent, gradient_output = native_gradients(*given)
     first_input, second_input, update_input = adam_parts(

time: 163 us -> 136 us (0.83)
  Pallas kernels: 157 us -> 130 us
    pallas_call x1, Pallas kernels: 151 us -> 123 us  [__call__(): pl.pallas_call(self.kernel, out_shape=[jax.ShapeDtypeStruct(*o) for o in...]
where the time goes in v3:
time: 136 us; the launch traced here: 135 us
  Pallas kernels  130 us (96%)
  local copies, waits for them, and re-layouts  4.1 us (3%)
  between operations  1.47 us (1%)
    pallas_call x1, Pallas kernels, __call__(): pl.pallas_call(self.kernel, out_shape=[jax.ShapeDtypeStruct(*o) for o in...  123 us
    pallas_call x1, Pallas kernels, update_all(): pl.pallas_call(update_kernel, out_shape=[jax.ShapeDtypeStruct((1, 1), f32...  6.82 us
    unnamed x2, local copies, waits for them, and re-layouts  4.1 us

profile of v3, /device:TPU:0, one launch (start us, length us, event | category | flops | bytes accessed | tf_op | source)
XLA Modules:
  0.0 135.4 jit_solution(5946174837781521611)
XLA Ops:
  1.3 1.9 %copy.34.tgt = bf16[4,384,83]{2,1,0:T(8,128)(2,1)} copy(bf16[4,384,83]{1,0,2:T(4,128)(2,1)} %param.17) | data formatting | bytes 509952 | tf_op args[1]
  3.2 2.2 %copy.33.x = bf16[4,384,227]{2,1,0:T(8,128)(2,1)} copy(bf16[4,384,227]{1,0,2:T(4,128)(2,1)} %param.16) | data formatting | bytes 1394688 | tf_op args[0]
  5.4 123.0 %train_step.1 = (f32[227,128]{1,0:T(8,128)}, f32[83,128]{1,0:T(8,128)}, f32[128,512]{1,0:T(8,128)}, bf16[128,1024]{1,0:T(8,128)(2,1)}, bf16[128,1024]{1,0:T(8,12...) custom-call(s32[1]{0:T(128)S(6)} %copy.35.count, bf16[4,384,227]{2,1,0:T(8,128)(2,1)} %copy.33.x, ...), custom_call_target="tpu_custom_call" | custom-call | tf_op jit(solution)/shard_map/train_step/pallas_call | solution.py:984
  128.4 6.8 %lamb.1 = (f32[1,1]{1,0:T(1,128)}, f32[227,128]{1,0:T(8,128)}, f32[6,128,512]{2,1,0:T(8,128)}, f32[83,128]{1,0:T(8,128)}, f32[227,128]{1,0:T(8,128)}, /*index=5*...) custom-call(f32[227,128]{1,0:T(8,128)} %get-tuple-element.41.g_in, ...), custom_call_target="tpu_custom_call" | custom-call | tf_op jit(solution)/shard_map/lamb/pallas_call | solution.py:1039

commit v4 on v3

--- a/solution.py
+++ b/solution.py
@@ -96,9 +96,14 @@
         at[axis] = self.to(axis, d)
         return (at["z"] * self.Y + at["y"], at["x"] * 2 + at["k"])
 
+    def others(self, axis):
+        if axis == "col":
+            return [(self.row, (self.col + d) % (2 * self.X)) for d in range(1, 2 * self.X)]
+        return [((self.row + d) % (self.Y * self.Z), self.col) for d in range(1, self.Y * self.Z)]
+
     def greet(self):
         sem = pltpu.get_barrier_semaphore()
-        peers = [self.peer(a, d) for a in "kxyz" for d in range(1, getattr(self, a.upper()))]
+        peers = self.others("col") + self.others("row")
         for peer in peers:
             pl.semaphore_signal(sem, inc=1, device_id=peer, device_id_type=MESH)
         return sem, len(peers)
@@ -160,27 +165,25 @@
 
 
 class Total:
-    AXES = "kxyz"
+    AXES = ("col", "row")
 
     @staticmethod
     def scratch(X, Y, Z):
-        many = 1 + X - 1 + Y - 1 + Z - 1
-        return [pltpu.VMEM((n, 8, 128), f32) for n in (2, X, Y, Z)] + [
+        many = 2 * X - 1 + Y * Z - 1
+        return [pltpu.VMEM((2 * X, 8, 128), f32), pltpu.VMEM((Y * Z, 8, 128), f32)] + [
             pltpu.VMEM((8, 128), f32),
             pltpu.SemaphoreType.DMA((many,)),
             pltpu.SemaphoreType.DMA((many,)),
         ]
 
     def __init__(self, place, refs):
-        self.p, self.bufs, (self.value, self.ss, self.rs) = place, dict(zip("kxyz", refs[:4])), refs[4:]
+        self.p, self.bufs, (self.value, self.ss, self.rs) = place, dict(zip(self.AXES, refs[:2])), refs[2:]
 
     def _copies(self, axis):
-        p, buf = self.p, self.bufs[axis]
-        base = sum(getattr(p, a.upper()) - 1 for a in self.AXES[: self.AXES.index(axis)])
-        here = buf.at[getattr(p, axis)]
-        for d in range(1, getattr(p, axis.upper())):
-            i = base + d - 1
-            yield remote(here, here, self.ss.at[i], self.rs.at[i], p.peer(axis, d))
+        p = self.p
+        base = 0 if axis == "col" else 2 * p.X - 1
+        here = self.bufs[axis].at[getattr(p, axis)]
+        return [remote(here, here, self.ss.at[base + i], self.rs.at[base + i], to) for i, to in enumerate(p.others(axis))]
 
     def start(self, axis):
         self.bufs[axis][getattr(self.p, axis)] = self.value[...]
@@ -192,12 +195,12 @@
             copy.wait_recv()
         buf = self.bufs[axis]
         value = buf[0]
-        for i in range(1, getattr(self.p, axis.upper())):
+        for i in range(1, buf.shape[0]):
             value = value + buf[i]
         self.value[...] = value
 
-    def drain(self, axes):
-        for axis in axes:
+    def drain(self):
+        for axis in self.AXES:
             for copy in self._copies(axis):
                 copy.wait_send()
 
@@ -390,6 +393,9 @@
             cmv=vm((C, N), bf16),
             cw=vm((C, 128), f32),
             cnt=vm((N, 128), f32),
+            fx=vm((N_IN, S, C), f32),
+            xb=vm((S * C, N_IN), bf16),
+            tb=vm((S * C, N_OUT), bf16),
             fp=vm((S * C, D), f32),
             gl=vm((S * C, D), bf16),
             tp=vm((S * C, D), f32),
@@ -470,8 +476,8 @@
         v = types.SimpleNamespace(**dict(zip(self.shapes, refs)))
         refs = refs[len(self.shapes) :]
         p = Place(self.n_row, self.n_col)
-        area_sum, stat_sum = Total(p, refs[:7]), Total(p, refs[7:14])
-        refs = refs[14:]
+        area_sum, stat_sum = Total(p, refs[:5]), Total(p, refs[5:10])
+        refs = refs[10:]
         for chunk in self.chunks:
             many = len(chunk.scratch())
             chunk.bind(p, refs[:many])
@@ -503,8 +509,9 @@
         W = lambda which: v.wlb[which]
         barrier = p.greet()
         own = ds(p.col * SH, SH)
-        loads = [pltpu.make_async_copy(wl.at[m], v.fp.at[m * SH : (m + 1) * SH, :], v.l_sem.at[m]) for m in range(6)]
-        for load in loads:
+        latents = [w for w in WIRE if isinstance(w, int)]
+        loads = {m: pltpu.make_async_copy(wl.at[m], v.fp.at[m * SH : (m + 1) * SH, :], v.l_sem.at[m]) for m in latents}
+        for load in loads.values():
             load.start()
 
         def turned(ref, n):
@@ -512,16 +519,15 @@
             v.tmp[0 : ref.shape[0], 0:SH] = ref[...]
             return jnp.transpose(v.tmp[0:n, 0:SH])
 
-        v.wib[own, :] = turned(wi, N_IN).astype(bf16)
-        v.wob[own, :] = turned(wo, N_OUT).astype(bf16)
-        for m, load in enumerate(loads):
-            load.wait()
-            v.wlb[m, own, :] = v.fp[m * SH : (m + 1) * SH, :].astype(bf16)
-        used = count[0]
-        area_row = area[...].reshape(1, C) * (lax.broadcasted_iota(jnp.int32, (1, C), 1) < used).astype(f32)
-        area_sum.value[...] = jnp.broadcast_to(jnp.sum(area_row), (8, 128))
-        pl.semaphore_wait(*barrier)
-
+        def w_ready(i):
+            m = WIRE[i]
+            if m == "in":
+                v.wib[own, :] = turned(wi, N_IN).astype(bf16)
+            elif m == "out":
+                v.wob[own, :] = turned(wo, N_OUT).astype(bf16)
+            else:
+                loads[m].wait()
+                v.wlb[m, own, :] = v.fp[m * SH : (m + 1) * SH, :].astype(bf16)
 
         def w_depart(*items):
             for i in items:
@@ -529,8 +535,27 @@
                 for d in hops:
                     w_copy(i, 1, d).start()
 
-        w_depart(0, 1, 2, 3)
-        area_sum.start("y")
+        w_ready(0)
+        w_ready(1)
+        pl.semaphore_wait(*barrier)
+        w_depart(0, 1)
+        for i in range(2, 8):
+            w_ready(i)
+            if i < 4:
+                w_depart(i)
+        used = count[0]
+        area_row = area[...].reshape(1, C) * (lax.broadcasted_iota(jnp.int32, (1, C), 1) < used).astype(f32)
+        area_sum.value[...] = jnp.broadcast_to(jnp.sum(area_row), (8, 128))
+        area_sum.start("col")
+
+        def by_cell(ref, n, out):
+            have = ref.shape[0]
+            v.fx[0:have] = ref[...].astype(f32)
+            v.fx[have:n] = jnp.zeros((n - have, S, C), f32)
+            for s in range(S):
+                out[s * C : (s + 1) * C, :] = jnp.transpose(v.fx[0:n, s, :]).astype(bf16)
+
+        by_cell(x, N_IN, v.xb)
 
         node_row = node[...].reshape(1, C)
         match = (lax.broadcasted_iota(jnp.int32, (N, C), 0) == node_row).astype(f32)
@@ -556,26 +581,32 @@
                 hit = lax.broadcasted_iota(jnp.int32, (E, 128), 1) + at == column
                 v.oh[:, base + at : base + at + 128] = hit.astype(f32).astype(bf16)
 
+        v.dp[...] = jnp.zeros((S * C, N_OUT), bf16)
+        v.loss[...] = jnp.zeros((8, 128), f32)
+
+        def encode(xx, s):
+            at, here, lanes = ds(s * C, C), ds(s * N, N), ds(xx * 2 * SH, 2 * SH)
+            pre = mm_nt(v.xb[at, :], v.wib[lanes, :])
+            v.fp[at, lanes] = pre
+            v.gl[at, lanes] = silu(pre).astype(bf16)
+            v.av[here, lanes] = (mm(v.nv[...], v.gl[at, lanes]) / v.cnt[:, 0:1]).astype(bf16)
+
+        def encode_all(xx):
+            def one(s, carry):
+                encode(xx, s)
+                return carry
+
+            lax.fori_loop(0, S, one, 0)
+
+        w_copy(0, 0).wait_recv()
+        encode_all(p.x)
+        w_forward(0)
+        by_cell(tgt, N_OUT, v.tb)
         table(snd[...], 0, R)
         table(rcv[...], R, Q)
-        v.dp[...] = jnp.zeros((S * C, N_OUT), bf16)
-        v.loss[...] = jnp.zeros((8, 128), f32)
-
-        w_forward(0)
-        w_get(0)
-
-        def encode(s, carry):
-            at = ds(s * C, C)
-            pre = mm_nt(x[s], v.wib[:, : self.c_in])
-            v.fp[at, :] = pre
-            v.gl[at, :] = silu(pre).astype(bf16)
-            here = ds(s * N, N)
-            v.av[here, :] = (mm(v.nv[...], v.gl[at, :]) / v.cnt[:, 0:1]).astype(bf16)
-            return carry
-
-        lax.fori_loop(0, S, encode, 0)
-        area_sum.finish("y")
-        area_sum.start("z")
+        for d in hops:
+            w_copy(0, 2, d).wait_recv()
+            encode_all(p.to("x", -d))
         w_forward(1)
         w_get(1)
         pre = mm(v.av[...], W(0))
@@ -617,8 +648,6 @@
         w_forward(2)
         w_forward(3)
         depart(1)
-        area_sum.finish("z")
-        area_sum.start("x")
         w_get(2)
         w_get(3)
 
@@ -706,12 +735,13 @@
             at, here = ds(s * C, C), ds(s * N, N)
             v.agb[here, :] = (col_last(0, s) * (1.0 / DEG)).astype(bf16)
             v.mnb[here, :] = (silu(v.sp[here, :]) + mm(v.agb[here, :], W(3))).astype(bf16)
+            pl.when(s == 0)(functools.partial(area_sum.finish, "row"))
             scale = 1.0 / (C_OUT * S * area_sum.value[0:1, 0:1])
             rows = mm(v.cm[...], v.mnb[here, :]).astype(bf16)
             pre = mm(rows, W(4)) + v.tp[at, :]
             v.tp[at, :] = pre
             v.go[at, :] = silu(pre).astype(bf16)
-            error = mm(v.go[at, :], v.wob[...])[:, :C_OUT] - tgt[s].astype(f32)
+            error = mm(v.go[at, :], v.wob[...])[:, :C_OUT] - v.tb[at, 0:C_OUT].astype(f32)
             weighted = v.cw[:, :C_OUT] * error
             v.loss[0:1, 0:C_OUT] = v.loss[0:1, 0:C_OUT] + jnp.sum(weighted * error, axis=0, keepdims=True)
             v.dp[at, 0:C_OUT] = (2.0 * weighted * scale).astype(bf16)
@@ -808,11 +838,10 @@
         def weights_rest():
             for i in (5, 6, 7):
                 w_forward(i)
-            area_sum.finish("x")
-            area_sum.start("k")
+            area_sum.finish("col")
+            area_sum.start("row")
             for i in (5, 6, 7):
                 w_get(i)
-            area_sum.finish("k")
 
         def partials_back(s):
             col_second(1, s)
@@ -820,18 +849,19 @@
 
         stage = lambda chunk, n: functools.partial(chunk.stage, n)
         line = [
+            (edges, 0),
             (edges_back, 3),
+            (stage(skips, 1), S + 2, None),
             (stage(decoders, 1), S + 2, None),
-            (edges, 0),
             (arrive, -2),
+            (functools.partial(col_second, 0), 0),
             (weights_rest, 1, None),
             (decoder_gradients, S + 1, None),
+            (lambda s: pl.when(s < S // 2)(functools.partial(pass_on, s)), 2),
+            (decode, 1),
+            (lambda s: pl.when(s >= S // 2)(functools.partial(pass_on, s)), 2),
             (partials_back, 4),
-            (pass_on, 2),
-            (stage(skips, 1), S + 1, None),
             (skip_back, S + 2, None),
-            (decode, 1),
-            (functools.partial(col_second, 0), 0),
             (stage(skips, 3), S + 5, None),
             (encode_back, 6),
             (stage(skips, 2), S + 3, None),
@@ -869,12 +899,7 @@
         receivers.stage(0)
         encoders.full[...] = mm_tn(v.av[...], v.d2b[...])
         encoders.stage(0)
-        inputs.full[:, self.c_in :] = jnp.zeros((D, N_IN - self.c_in), f32)
-        for s in range(S):
-            grad = mm_tn(v.dt[s * C : (s + 1) * C, :], x[s])
-            if s:
-                grad = grad + inputs.full[:, : self.c_in]
-            inputs.full[:, : self.c_in] = grad
+        inputs.full[...] = mm_tn(v.dt[...], v.xb[...])
         inputs.stage(0)
         senders.stage(1)
         encoders.stage(1)
@@ -907,50 +932,46 @@
         note(7, skips.piece[:, D : D + N_OUT], edge, slice(N_IN, N_IN + N_OUT))
         senders.stage(2)
         encoders.stage(2)
+        receivers.stage(2)
+        inputs.stage(2)
+        senders.stage(3)
+        encoders.stage(3)
         decoders.stage(4)
         note_latent(4, decoders.piece[:, 0:D])
         note_latent(3, decoders.piece[:, D : 2 * D])
-        receivers.stage(2)
-        inputs.stage(2)
+        inputs.stage(3)
+        receivers.stage(3)
         skips.stage(5)
-        senders.stage(3)
-        encoders.stage(3)
-        receivers.stage(3)
-        inputs.stage(3)
-        decoders.stage(5)
         senders.stage(4)
         note_latent(1, senders.piece[...])
         encoders.stage(4)
         note_latent(0, encoders.piece[...])
+        inputs.stage(4)
+        note(0, inputs.piece[...], edge, slice(0, N_IN))
         receivers.stage(4)
         note_latent(2, receivers.piece[...])
-        inputs.stage(4)
-        note(0, inputs.piece[...], edge, slice(0, N_IN))
-        stat_sum.start("k")
+        stat_sum.start("col")
+        decoders.stage(5)
         skips.stage(6)
         g_skip[...] = skips.out[:, :D]
         g_out[...] = jnp.transpose(skips.out[:, D : D + N_OUT])[: g_out.shape[0], :]
-        stat_sum.finish("k")
-        stat_sum.start("x")
+        senders.stage(5)
+        encoders.stage(5)
+        stat_sum.finish("col")
+        stat_sum.start("row")
+        inputs.stage(5)
+        receivers.stage(5)
         decoders.stage(6)
         g_two[...] = decoders.out[...]
-        senders.stage(5)
-        encoders.stage(5)
-        stat_sum.finish("x")
-        stat_sum.start("z")
-        receivers.stage(5)
-        inputs.stage(5)
         senders.stage(6)
         g_three[:, 0:D] = senders.out[...]
         encoders.stage(6)
         g_four[...] = encoders.out[...]
-        stat_sum.finish("z")
-        stat_sum.start("y")
+        inputs.stage(6)
+        g_in[...] = jnp.transpose(inputs.out[...])[: g_in.shape[0], :]
         receivers.stage(6)
         g_three[:, D : 2 * D] = receivers.out[...]
-        inputs.stage(6)
-        g_in[...] = jnp.transpose(inputs.out[...])[: g_in.shape[0], :]
-        stat_sum.finish("y")
+        stat_sum.finish("row")
         stats[...] = jnp.where(row < 2, stat_sum.value[...], stat_sum.value[...] / (C_OUT * S * area_sum.value[...]))
 
         for i in range(8):
@@ -972,8 +993,8 @@
                 pk(1, s, xx).wait_send()
             for d in hops:
                 px(1, s, d).wait_send()
-        area_sum.drain("kxyz")
-        stat_sum.drain("kxyz")
+        area_sum.drain()
+        stat_sum.drain()
         for chunk in self.chunks:
             chunk.drain()
 
@@ -1057,6 +1078,7 @@
 
 def kernel_body(mesh, step, inputs, targets, cell_area, cell_count, cell_node, edge_senders, edge_receivers, *states):
     states = [a.T if i % 3 == 2 else a for i, a in enumerate(states)]
+    inputs, targets = (a.transpose(2, 0, 1) for a in (inputs, targets))
     grads = step(cell_count, inputs, targets, cell_area, cell_node, edge_senders[None, :], edge_receivers[None, :], *states)
     loss, *outs, norms = update_all(grads, states)
     outs = [a.T if i % 3 == 2 else a for i, a in enumerate(outs)]

time: 136 us -> 134 us (0.985)
  local copies, waits for them, and re-layouts: 4.1 us -> 0 us
  Pallas kernels: 130 us -> 132 us
    unnamed x2 -> x0, local copies, waits for them, and re-layouts: 4.1 us -> none
    pallas_call x1, Pallas kernels: 123 us -> 125 us  [__call__(): pl.pallas_call(self.kernel, out_shape=[jax.ShapeDtypeStruct(*o) for o in...]
where the time goes in v4:
time: 134 us; the launch traced here: 133 us
  Pallas kernels  132 us (99%)
  between operations  1.47 us (1%)
    pallas_call x1, Pallas kernels, __call__(): pl.pallas_call(self.kernel, out_shape=[jax.ShapeDtypeStruct(*o) for o in...  125 us
    pallas_call x1, Pallas kernels, update_all(): pl.pallas_call(update_kernel, out_shape=[jax.ShapeDtypeStruct((1, 1), f32...  6.82 us

profile of v4, /device:TPU:0, one launch (start us, length us, event | category | flops | bytes accessed | tf_op | source)
XLA Modules:
  0.0 133.3 jit_solution(9990316544253567036)
XLA Ops:
  1.3 125.0 %train_step.1 = (f32[227,128]{1,0:T(8,128)}, f32[83,128]{1,0:T(8,128)}, f32[128,512]{1,0:T(8,128)}, bf16[128,1024]{1,0:T(8,128)(2,1)}, bf16[128,1024]{1,0:T(8,12...) custom-call(s32[1]{0:T(128)S(6)} %copy.33.count, bf16[227,4,384]{2,1,0:T(4,128)(2,1)} %bitcast.13, ...), custom_call_target="tpu_custom_call" | custom-call | tf_op jit(solution)/shard_map/train_step/pallas_call | solution.py:1005
  126.3 6.8 %lamb.1 = (f32[1,1]{1,0:T(1,128)}, f32[227,128]{1,0:T(8,128)}, f32[6,128,512]{2,1,0:T(8,128)}, f32[83,128]{1,0:T(8,128)}, f32[227,128]{1,0:T(8,128)}, /*index=5*...) custom-call(f32[227,128]{1,0:T(8,128)} %get-tuple-element.41.g_in, ...), custom_call_target="tpu_custom_call" | custom-call | tf_op jit(solution)/shard_map/lamb/pallas_call | solution.py:1060

commit v5 on v4

--- a/solution.py
+++ b/solution.py
@@ -96,14 +96,9 @@
         at[axis] = self.to(axis, d)
         return (at["z"] * self.Y + at["y"], at["x"] * 2 + at["k"])
 
-    def others(self, axis):
-        if axis == "col":
-            return [(self.row, (self.col + d) % (2 * self.X)) for d in range(1, 2 * self.X)]
-        return [((self.row + d) % (self.Y * self.Z), self.col) for d in range(1, self.Y * self.Z)]
-
     def greet(self):
         sem = pltpu.get_barrier_semaphore()
-        peers = self.others("col") + self.others("row")
+        peers = [self.peer(a, d) for a in "kxyz" for d in range(1, getattr(self, a.upper()))]
         for peer in peers:
             pl.semaphore_signal(sem, inc=1, device_id=peer, device_id_type=MESH)
         return sem, len(peers)
@@ -165,25 +160,27 @@
 
 
 class Total:
-    AXES = ("col", "row")
+    AXES = "kxyz"
 
     @staticmethod
     def scratch(X, Y, Z):
-        many = 2 * X - 1 + Y * Z - 1
-        return [pltpu.VMEM((2 * X, 8, 128), f32), pltpu.VMEM((Y * Z, 8, 128), f32)] + [
+        many = 1 + X - 1 + Y - 1 + Z - 1
+        return [pltpu.VMEM((n, 8, 128), f32) for n in (2, X, Y, Z)] + [
             pltpu.VMEM((8, 128), f32),
             pltpu.SemaphoreType.DMA((many,)),
             pltpu.SemaphoreType.DMA((many,)),
         ]
 
     def __init__(self, place, refs):
-        self.p, self.bufs, (self.value, self.ss, self.rs) = place, dict(zip(self.AXES, refs[:2])), refs[2:]
+        self.p, self.bufs, (self.value, self.ss, self.rs) = place, dict(zip("kxyz", refs[:4])), refs[4:]
 
     def _copies(self, axis):
-        p = self.p
-        base = 0 if axis == "col" else 2 * p.X - 1
-        here = self.bufs[axis].at[getattr(p, axis)]
-        return [remote(here, here, self.ss.at[base + i], self.rs.at[base + i], to) for i, to in enumerate(p.others(axis))]
+        p, buf = self.p, self.bufs[axis]
+        base = sum(getattr(p, a.upper()) - 1 for a in self.AXES[: self.AXES.index(axis)])
+        here = buf.at[getattr(p, axis)]
+        for d in range(1, getattr(p, axis.upper())):
+            i = base + d - 1
+            yield remote(here, here, self.ss.at[i], self.rs.at[i], p.peer(axis, d))
 
     def start(self, axis):
         self.bufs[axis][getattr(self.p, axis)] = self.value[...]
@@ -195,12 +192,12 @@
             copy.wait_recv()
         buf = self.bufs[axis]
         value = buf[0]
-        for i in range(1, buf.shape[0]):
+        for i in range(1, getattr(self.p, axis.upper())):
             value = value + buf[i]
         self.value[...] = value
 
-    def drain(self):
-        for axis in self.AXES:
+    def drain(self, axes):
+        for axis in axes:
             for copy in self._copies(axis):
                 copy.wait_send()
 
@@ -476,8 +473,8 @@
         v = types.SimpleNamespace(**dict(zip(self.shapes, refs)))
         refs = refs[len(self.shapes) :]
         p = Place(self.n_row, self.n_col)
-        area_sum, stat_sum = Total(p, refs[:5]), Total(p, refs[5:10])
-        refs = refs[10:]
+        area_sum, stat_sum = Total(p, refs[:7]), Total(p, refs[7:14])
+        refs = refs[14:]
         for chunk in self.chunks:
             many = len(chunk.scratch())
             chunk.bind(p, refs[:many])
@@ -546,7 +543,7 @@
         used = count[0]
         area_row = area[...].reshape(1, C) * (lax.broadcasted_iota(jnp.int32, (1, C), 1) < used).astype(f32)
         area_sum.value[...] = jnp.broadcast_to(jnp.sum(area_row), (8, 128))
-        area_sum.start("col")
+        area_sum.start("y")
 
         def by_cell(ref, n, out):
             have = ref.shape[0]
@@ -609,6 +606,8 @@
             encode_all(p.to("x", -d))
         w_forward(1)
         w_get(1)
+        area_sum.finish("y")
+        area_sum.start("z")
         pre = mm(v.av[...], W(0))
         v.sp[...] = pre
         v.mlb[...] = silu(pre).astype(bf16)
@@ -648,6 +647,8 @@
         w_forward(2)
         w_forward(3)
         depart(1)
+        area_sum.finish("z")
+        area_sum.start("k")
         w_get(2)
         w_get(3)
 
@@ -735,7 +736,6 @@
             at, here = ds(s * C, C), ds(s * N, N)
             v.agb[here, :] = (col_last(0, s) * (1.0 / DEG)).astype(bf16)
             v.mnb[here, :] = (silu(v.sp[here, :]) + mm(v.agb[here, :], W(3))).astype(bf16)
-            pl.when(s == 0)(functools.partial(area_sum.finish, "row"))
             scale = 1.0 / (C_OUT * S * area_sum.value[0:1, 0:1])
             rows = mm(v.cm[...], v.mnb[here, :]).astype(bf16)
             pre = mm(rows, W(4)) + v.tp[at, :]
@@ -838,8 +838,7 @@
         def weights_rest():
             for i in (5, 6, 7):
                 w_forward(i)
-            area_sum.finish("col")
-            area_sum.start("row")
+            area_sum.finish("x")
             for i in (5, 6, 7):
                 w_get(i)
 
@@ -856,10 +855,10 @@
             (arrive, -2),
             (functools.partial(col_second, 0), 0),
             (weights_rest, 1, None),
-            (decoder_gradients, S + 1, None),
             (lambda s: pl.when(s < S // 2)(functools.partial(pass_on, s)), 2),
             (decode, 1),
             (lambda s: pl.when(s >= S // 2)(functools.partial(pass_on, s)), 2),
+            (decoder_gradients, S + 1, None),
             (partials_back, 4),
             (skip_back, S + 2, None),
             (stage(skips, 3), S + 5, None),
@@ -874,6 +873,8 @@
         by_rows(S * C, 512, skip)
         arrive(1)
         depart(3)
+        area_sum.finish("k")
+        area_sum.start("x")
 
         def turn(i, carry):
             for todo, behind, *once in line:
@@ -897,6 +898,7 @@
         senders.stage(0)
         receivers.full[...] = mm_tn(v.mlb[...], v.drb[...])
         receivers.stage(0)
+        decoders.stage(3)
         encoders.full[...] = mm_tn(v.av[...], v.d2b[...])
         encoders.stage(0)
         inputs.full[...] = mm_tn(v.dt[...], v.xb[...])
@@ -905,7 +907,6 @@
         encoders.stage(1)
         receivers.stage(1)
         inputs.stage(1)
-        decoders.stage(3)
 
         for load in states:
             load.wait()
@@ -930,15 +931,15 @@
         skips.stage(4)
         note_latent(5, skips.piece[:, 0:D])
         note(7, skips.piece[:, D : D + N_OUT], edge, slice(N_IN, N_IN + N_OUT))
+        decoders.stage(4)
+        note_latent(4, decoders.piece[:, 0:D])
+        note_latent(3, decoders.piece[:, D : 2 * D])
         senders.stage(2)
         encoders.stage(2)
         receivers.stage(2)
         inputs.stage(2)
         senders.stage(3)
         encoders.stage(3)
-        decoders.stage(4)
-        note_latent(4, decoders.piece[:, 0:D])
-        note_latent(3, decoders.piece[:, D : 2 * D])
         inputs.stage(3)
         receivers.stage(3)
         skips.stage(5)
@@ -950,15 +951,17 @@
         note(0, inputs.piece[...], edge, slice(0, N_IN))
         receivers.stage(4)
         note_latent(2, receivers.piece[...])
-        stat_sum.start("col")
+        stat_sum.start("k")
         decoders.stage(5)
+        stat_sum.finish("k")
+        stat_sum.start("x")
         skips.stage(6)
         g_skip[...] = skips.out[:, :D]
         g_out[...] = jnp.transpose(skips.out[:, D : D + N_OUT])[: g_out.shape[0], :]
         senders.stage(5)
         encoders.stage(5)
-        stat_sum.finish("col")
-        stat_sum.start("row")
+        stat_sum.finish("x")
+        stat_sum.start("z")
         inputs.stage(5)
         receivers.stage(5)
         decoders.stage(6)
@@ -967,11 +970,13 @@
         g_three[:, 0:D] = senders.out[...]
         encoders.stage(6)
         g_four[...] = encoders.out[...]
+        stat_sum.finish("z")
+        stat_sum.start("y")
         inputs.stage(6)
         g_in[...] = jnp.transpose(inputs.out[...])[: g_in.shape[0], :]
         receivers.stage(6)
         g_three[:, D : 2 * D] = receivers.out[...]
-        stat_sum.finish("row")
+        stat_sum.finish("y")
         stats[...] = jnp.where(row < 2, stat_sum.value[...], stat_sum.value[...] / (C_OUT * S * area_sum.value[...]))
 
         for i in range(8):
@@ -993,8 +998,8 @@
                 pk(1, s, xx).wait_send()
             for d in hops:
                 px(1, s, d).wait_send()
-        area_sum.drain()
-        stat_sum.drain()
+        area_sum.drain("kxyz")
+        stat_sum.drain("kxyz")
         for chunk in self.chunks:
             chunk.drain()
 

time: 134 us -> 129 us (0.963)
  Pallas kernels: 132 us -> 127 us
    pallas_call x1, Pallas kernels: 125 us -> 120 us  [__call__(): pl.pallas_call(self.kernel, out_shape=[jax.ShapeDtypeStruct(*o) for o in...]
where the time goes in v5:
time: 129 us
  Pallas kernels  127 us (98%)
  between operations  1.47 us (1%)
    pallas_call x1, Pallas kernels, __call__(): pl.pallas_call(self.kernel, out_shape=[jax.ShapeDtypeStruct(*o) for o in...  120 us
    pallas_call x1, Pallas kernels, update_all(): pl.pallas_call(update_kernel, out_shape=[jax.ShapeDtypeStruct((1, 1), f32...  6.82 us

profile of v5, /device:TPU:0, one launch (start us, length us, event | category | flops | bytes accessed | tf_op | source)
XLA Modules:
  0.0 128.7 jit_solution(10481646236258021509)
XLA Ops:
  1.3 120.5 %train_step.1 = (f32[227,128]{1,0:T(8,128)}, f32[83,128]{1,0:T(8,128)}, f32[128,512]{1,0:T(8,128)}, bf16[128,1024]{1,0:T(8,128)(2,1)}, bf16[128,1024]{1,0:T(8,12...) custom-call(s32[1]{0:T(128)S(6)} %copy.33.count, bf16[227,4,384]{2,1,0:T(4,128)(2,1)} %bitcast.13, ...), custom_call_target="tpu_custom_call" | custom-call | tf_op jit(solution)/shard_map/train_step/pallas_call | solution.py:1010
  121.8 6.8 %lamb.1 = (f32[1,1]{1,0:T(1,128)}, f32[227,128]{1,0:T(8,128)}, f32[6,128,512]{2,1,0:T(8,128)}, f32[83,128]{1,0:T(8,128)}, f32[227,128]{1,0:T(8,128)}, /*index=5*...) custom-call(f32[227,128]{1,0:T(8,128)} %get-tuple-element.41.g_in, ...), custom_call_target="tpu_custom_call" | custom-call | tf_op jit(solution)/shard_map/lamb/pallas_call | solution.py:1065

commit v6 on v5

--- a/solution.py
+++ b/solution.py
@@ -1020,11 +1020,16 @@
 
 def update_kernel(g_in, g_out, g_skip, g_two, g_three, g_four, stats, wi, wl, wo, mi, mal, mo, si, sal, so, *refs):
     loss, *outs, norms = refs[:17]
-    in_buf, out_buf, low_buf, in_sem, out_sem = refs[17:]
+    in_buf, out_buf, low_buf, skip_buf, two_buf, three_buf, four_buf, in_sem, out_sem, g_sem = refs[17:]
     SH, D = g_skip.shape
     loads = [[pltpu.make_async_copy(a.at[m], in_buf.at[j, m], in_sem.at[j, m]) for j, a in enumerate((wl, mal, sal))] for m in range(6)]
     order = (5, 4, 3, 2, 1, 0)
+    pairs = ((g_skip, skip_buf), (g_two, two_buf), (g_three, three_buf), (g_four, four_buf))
+    takes = [pltpu.make_async_copy(ref, buf, g_sem.at[i]) for i, (ref, buf) in enumerate(pairs)]
+    first_use = {5: 0, 4: 1, 2: 2, 0: 3}
     for m in order:
+        if m in first_use:
+            takes[first_use[m]].start()
         for load in loads[m]:
             load.start()
     root = jnp.sqrt(stats[...])
@@ -1037,9 +1042,15 @@
         master = weight - learn_rate * ratio * update
         return gradient, first, second, master, master.astype(bf16)
 
-    grads = {5: (g_skip, 0), 4: (g_two, 0), 3: (g_two, D), 2: (g_three, D), 1: (g_three, 0), 0: (g_four, 0)}
+    for j, result in enumerate(step(0, wi[...], g_in[...], mi[...], si[...])):
+        outs[3 * j][...] = result
+    for j, result in enumerate(step(7, wo[...], g_out[...], mo[...], so[...])):
+        outs[3 * j + 2][...] = result
+    grads = {5: (skip_buf, 0), 4: (two_buf, 0), 3: (two_buf, D), 2: (three_buf, D), 1: (three_buf, 0), 0: (four_buf, 0)}
     stores = []
     for m in order:
+        if m in first_use:
+            takes[first_use[m]].wait()
         for load in loads[m]:
             load.wait()
         ref, at = grads[m]
@@ -1049,10 +1060,6 @@
             buf[...] = result
             stores.append(pltpu.make_async_copy(buf, outs[3 * j + 1].at[m], out_sem.at[j, m]))
             stores[-1].start()
-    for j, result in enumerate(step(0, wi[...], g_in[...], mi[...], si[...])):
-        outs[3 * j][...] = result
-    for j, result in enumerate(step(7, wo[...], g_out[...], mo[...], so[...])):
-        outs[3 * j + 2][...] = result
     for store in stores:
         store.wait()
 
@@ -1067,14 +1074,19 @@
         out_shape=[jax.ShapeDtypeStruct((1, 1), f32)]
         + [jax.ShapeDtypeStruct(s, k) for k in kinds for s in shapes]
         + [jax.ShapeDtypeStruct((2, 8), f32)],
-        in_specs=[vm] * 7 + [vm, hbm, vm] * 3,
+        in_specs=[vm, vm, hbm, hbm, hbm, hbm, vm] + [vm, hbm, vm] * 3,
         out_specs=[vm] + [vm, hbm, vm] * 5 + [vm],
         scratch_shapes=[
             pltpu.VMEM((3, n, SH, D), f32),
             pltpu.VMEM((4, n, SH, D), f32),
             pltpu.VMEM((n, SH, D), bf16),
+            pltpu.VMEM((SH, D), f32),
+            pltpu.VMEM((SH, 2 * D), bf16),
+            pltpu.VMEM((SH, 2 * D), bf16),
+            pltpu.VMEM((SH, D), bf16),
             pltpu.SemaphoreType.DMA((3, n)),
             pltpu.SemaphoreType.DMA((5, n)),
+            pltpu.SemaphoreType.DMA((4,)),
         ],
         name="lamb",
         compiler_params=pltpu.CompilerParams(vmem_limit_bytes=67043328),

time: 129 us -> 130 us (level)
  no operation moved by 1% of the time
where the time goes in v6:
time: 130 us; the launch traced here: 129 us
  Pallas kernels  128 us (98%)
  between operations  1.47 us (1%)
    pallas_call x1, Pallas kernels, __call__(): pl.pallas_call(self.kernel, out_shape=[jax.ShapeDtypeStruct(*o) for o in...  120 us
    pallas_call x1, Pallas kernels, update_all(): pl.pallas_call(update_kernel, out_shape=[jax.ShapeDtypeStruct((1, 1), f32...  7.5 us

profile of v6, /device:TPU:0, one launch (start us, length us, event | category | flops | bytes accessed | tf_op | source)
XLA Modules:
  0.0 129.4 jit_solution(11906191925285264960)
XLA Ops:
  1.3 120.5 %train_step.1 = (f32[227,128]{1,0:T(8,128)}, f32[83,128]{1,0:T(8,128)}, f32[128,512]{1,0:T(8,128)}, bf16[128,1024]{1,0:T(8,128)(2,1)}, bf16[128,1024]{1,0:T(8,12...) custom-call(s32[1]{0:T(128)S(6)} %copy.33.count, bf16[227,4,384]{2,1,0:T(4,128)(2,1)} %bitcast.13, ...), custom_call_target="tpu_custom_call" | custom-call | tf_op jit(solution)/shard_map/train_step/pallas_call | solution.py:1010
  121.8 7.5 %lamb.1 = (f32[1,1]{1,0:T(1,128)}, f32[227,128]{1,0:T(8,128)}, f32[6,128,512]{2,1,0:T(8,128)}, f32[83,128]{1,0:T(8,128)}, f32[227,128]{1,0:T(8,128)}, /*index=5*...) custom-call(f32[227,128]{1,0:T(8,128)} %get-tuple-element.41.g_in, ...), custom_call_target="tpu_custom_call" | custom-call | tf_op jit(solution)/shard_map/lamb/pallas_call | solution.py:1072
